TPU v7x, 32 devices: a whole 2x2x4 slice. The times are simulated.
32 devices in a mesh: seq: 8 (over z, y), tp: 4 (over x, core).
Axes of the slice: x: 2, y: 2, z: 4, core: 2. Of those that a mesh axis runs over, the one named last changes fastest.
Arguments:
- queries: bfloat16 [1, 2048, 4096], P(None, 'seq', 'tp'), may hold values from -13 to 13
- key_rows: bfloat16 [1, 2048, 2048], P(None, 'seq', 'tp'), may hold values from -13 to 13
- value_rows: bfloat16 [1, 2048, 2048], P(None, 'seq', 'tp'), may hold values from -6 to 6
- residual: bfloat16 [1, 2048, 3584], P(None, 'seq', 'tp'), may hold values from -6 to 6
- out_weight: bfloat16 [4096, 3584], P('tp')
- post_scale: float32 [3584], P('tp'), may hold values from 0.1 to 1.9
- lengths: int32 [1], replicated, may hold values from 512 to 2047
- owners: int32 [1, 8], replicated, may hold values from 0 to 7, each once within a row
Outputs:
- hidden_out: bfloat16 [1, 2048, 3584], P(None, 'seq', 'tp')
- cache_keys: bfloat16 [1, 4096, 2048], P(None, 'seq', 'tp')
- cache_values: bfloat16 [1, 4096, 2048], P(None, 'seq', 'tp')
Inputs may be any that keep to these rules, and one draw needn't show every extreme that they name: Each row of owners names every number from 0 to 7 once.
All inputs are finite; a program needn't handle non-finite values.
Results may differ from a plain program's by a relative error of at most 0.0083.
Values may be sent and summed in bfloat16 or wider, within the bound.
A program may use at most 64 MiB of HBM per device.

v0:
```python
import functools

import jax
import jax.numpy as jnp
from jax import lax
from jax.experimental import pallas as pl
from jax.experimental.pallas import tpu as pltpu
from jax.sharding import PartitionSpec as P

D = 3584
HD = 256
WINDOW = 4096
MESH = pl.DeviceIdType.MESH
LOG2E = 1.4426950408889634
ROWS = 128


soft_cap = 50.0
norm_eps = 1e-06


def shifted(x, axis, by):
    peers = lax.axis_size(axis)
    pairs = [(i, i + by) for i in range(peers) if 0 <= i + by < peers]
    return lax.ppermute(x, axis, pairs)


def attend_block(grouped, block_keys, block_values, query_pos, key_pos, state_pair):
    numerator, denominator = state_pair
    seq_count, query_count, kv_local, group_size, head_size = grouped.shape
    keyed_rows = block_keys.reshape(seq_count, block_keys.shape[1], kv_local, head_size)
    valued_rows = block_values.reshape(seq_count, block_values.shape[1], kv_local, head_size)
    scores = jnp.einsum(
        "sqhgd,skhd->shgqk", grouped, keyed_rows, preferred_element_type=jnp.float32
    ) * head_size ** (-0.5)
    capped = soft_cap * jnp.tanh(scores / soft_cap)
    spread = query_pos[:, None] - key_pos[None, :]
    live_mask = (spread >= 0) & (spread < WINDOW) & (key_pos[None, :] >= 0)
    weights = jnp.where(live_mask, jnp.exp(capped), jnp.zeros_like(capped))
    denominator = denominator + jnp.sum(weights, axis=-1)
    numerator = numerator + jnp.einsum(
        "shgqk,skhd->sqhgd",
        weights.astype(jnp.bfloat16),
        valued_rows,
        preferred_element_type=jnp.float32,
    )
    return (numerator, denominator)


def reorder_blocks(blocked, ordering):
    return blocked[ordering]


def local(queries, key_rows, value_rows, residual, out_weight, post_scale, lengths, owners):
    seq_count, shard_len, query_width = queries.shape
    seq_size = lax.axis_size("seq")
    if (
        seq_count == 1 and lax.axis_size("tp") == 4 and seq_size % 2 == 0
        and seq_size * shard_len <= WINDOW
    ):
        return fused(
            seq_size, queries, key_rows, value_rows, residual, out_weight, post_scale, lengths,
            owners,
        )
    kv_width = key_rows.shape[2]
    kv_local = kv_width // HD
    group_size = query_width // kv_width
    grouped = queries.reshape(seq_count, shard_len, kv_local, group_size, HD)
    position = lax.axis_index("seq")
    seq_devices = lax.axis_size("seq")
    offsets = jnp.arange(shard_len, dtype=jnp.int32)
    query_pos = position * shard_len + offsets
    numerator = jnp.zeros((seq_count, shard_len, kv_local, group_size, HD), jnp.float32)
    denominator = jnp.zeros((seq_count, kv_local, group_size, shard_len), jnp.float32)
    state_pair = attend_block(
        grouped, key_rows, value_rows, query_pos, query_pos, (numerator, denominator)
    )
    hop_count = min(WINDOW // shard_len, seq_devices - 1)
    arrived = []
    current = (key_rows, value_rows)
    for hop_index in range(1, hop_count + 1):
        current = shifted((current[0], current[1]), "seq", 1)
        arrived.append((hop_index, current))
        if len(arrived) == 2 or hop_index == hop_count:
            ordered = arrived[::-1]
            block_keys = jnp.concatenate([member[1][0] for member in ordered], axis=1)
            block_values = jnp.concatenate([member[1][1] for member in ordered], axis=1)
            block_pos = jnp.concatenate(
                [(position - member[0]) * shard_len + offsets for member in ordered]
            )
            state_pair = attend_block(
                grouped, block_keys, block_values, query_pos, block_pos, state_pair
            )
            arrived = []
    numerator, denominator = state_pair
    attended = (numerator / jnp.transpose(denominator, (0, 3, 1, 2))[..., None]).astype(
        jnp.bfloat16
    )
    partial_value = jnp.dot(
        attended.reshape(seq_count * shard_len, query_width),
        out_weight,
        preferred_element_type=jnp.float32,
    )
    partial_value = partial_value.reshape(seq_count, shard_len, out_weight.shape[1])
    branch = lax.psum_scatter(partial_value, "tp", scatter_dimension=2, tiled=True)
    squares = lax.psum(jnp.sum(branch * branch, axis=-1), "tp")
    normed = branch * lax.rsqrt(squares / D + norm_eps)[..., None] * post_scale
    hidden_out = (residual.astype(jnp.float32) + normed).astype(jnp.bfloat16)
    block_rows = shard_len // seq_devices
    slot_span = WINDOW // shard_len
    live_rows = (query_pos[None, :] >= lengths[:, None] - WINDOW) & (
        query_pos[None, :] < lengths[:, None]
    )
    kept_keys = jnp.where(live_rows[..., None], key_rows, jnp.zeros_like(key_rows))
    kept_values = jnp.where(live_rows[..., None], value_rows, jnp.zeros_like(value_rows))
    devices = jnp.arange(seq_devices, dtype=jnp.int32)
    matches = owners[:, :, None] == devices[None, None, :]
    inverse = jnp.sum(
        jnp.where(matches, devices[None, :, None], jnp.zeros_like(devices)[None, :, None]), axis=1
    )
    outgoing_keys = jax.vmap(reorder_blocks)(
        kept_keys.reshape(seq_count, seq_devices, block_rows, kv_width), inverse
    )
    outgoing_values = jax.vmap(reorder_blocks)(
        kept_values.reshape(seq_count, seq_devices, block_rows, kv_width), inverse
    )
    incoming = (
        lax.all_to_all(outgoing_keys, "seq", split_axis=1, concat_axis=1, tiled=True),
        lax.all_to_all(outgoing_values, "seq", split_axis=1, concat_axis=1, tiled=True),
    )
    selector = (
        devices[None, :] % slot_span == jnp.arange(slot_span, dtype=jnp.int32)[:, None]
    ).astype(jnp.bfloat16)
    cache_keys = (
        jnp.einsum("md,sdbf->smbf", selector, incoming[0], preferred_element_type=jnp.float32)
        .astype(jnp.bfloat16)
        .reshape(seq_count, slot_span * block_rows, kv_width)
    )
    cache_values = (
        jnp.einsum("md,sdbf->smbf", selector, incoming[1], preferred_element_type=jnp.float32)
        .astype(jnp.bfloat16)
        .reshape(seq_count, slot_span * block_rows, kv_width)
    )
    return (hidden_out, cache_keys, cache_values)


def layer_kernel(
    n, q_hbm, k_hbm, v_hbm, res_hbm, scale_hbm, len_ref, own_hbm, w_ref,
    hid_hbm, ck_hbm, cv_hbm,
    hid_ref, ck_ref, cv_ref, q_ref, res_ref, scale_ref, own_ref, kstage, vstage, kgot, vgot,
    kbuf, vbuf, wbuf, acc, den, att, to_sib, to_x, to_sib2, from_sib, from_x, from_sib2,
    total, sq_out, sq_in,
    in_sem, send_sem, recv_sem, w_sem, rs_send, rs_recv, sq_send, sq_recv, cache_send, cache_recv, out_sem,
):
    nz = n // 2
    me = lax.axis_index("seq")
    t = lax.axis_index("tp")
    z, y = me // 2, me % 2
    x, c = t // 2, t % 2
    sib = x * 2 + (1 - c)
    across = (1 - x) * 2 + c
    diagonal = (1 - x) * 2 + (1 - c)
    shard = q_ref.shape[0]
    heads = q_ref.shape[1] // HD
    kv_width = k_hbm.shape[1]
    group = q_ref.shape[1] // kv_width
    block_rows = shard // n
    bufs = (kbuf, vbuf)
    loads = [
        pltpu.make_async_copy(src, dst, in_sem.at[i])
        for i, (src, dst) in enumerate(
            (
                (k_hbm, kbuf.at[me]), (v_hbm, vbuf.at[me]), (q_hbm, q_ref), (own_hbm, own_ref),
                (res_hbm, res_ref), (scale_hbm, scale_ref),
            )
        )
    ]
    for load in loads:
        load.start()

    def w_copy(f):
        return pltpu.make_async_copy(
            w_ref.at[:, pl.ds(f * res_ref.shape[1], res_ref.shape[1])], wbuf.at[f], w_sem.at[f]
        )

    partner = z * 2 + (1 - y)
    barrier = pltpu.get_barrier_semaphore()
    for peer in (sib, across, diagonal):
        pl.semaphore_signal(barrier, inc=1, device_id={"tp": peer}, device_id_type=MESH)
    for hop in range(1, n):
        pl.semaphore_signal(
            barrier, inc=1, device_id={"seq": lax.rem(me + hop, n)}, device_id_type=MESH
        )
    pl.semaphore_wait(barrier, n + 2)

    def routes(zo, yo, h):
        special = ((zo == 0) & (yo == 0)) if h == 1 else False
        line = (yo == y) | special
        crossing = (yo == y) & (zo + y <= z) & ((zo == z) | jnp.logical_not(special))
        origin = zo * 2 + yo
        plan = ((line & (zo <= z) & (z < nz - 1), me + 2), (crossing, partner))
        out = []
        for way, (go, to) in enumerate(plan):
            copy = pltpu.make_async_remote_copy(
                src_ref=bufs[h].at[origin],
                dst_ref=bufs[h].at[origin],
                send_sem=send_sem.at[origin, h, way],
                recv_sem=recv_sem.at[origin, h],
                device_id={"seq": to},
                device_id_type=MESH,
            )
            out.append((go, copy))
        return out

    def start(zo, yo, h):
        for go, copy in routes(zo, yo, h):
            pl.when(go)(copy.start)

    def handle(zo, yo, h):
        routes(zo, yo, h)[0][1].wait_recv()
        start(zo, yo, h)

    for h in (0, 1):
        loads[h].wait()
        start(z, y, h)
    for f in range(4):
        w_copy(f).start()
    loads[2].wait()
    loads[3].wait()

    def attend(keys, values, masked):
        for h in range(heads):
            cols = pl.ds((h // group) * HD, HD)
            s = lax.dot_general(
                q_ref[:, h * HD : (h + 1) * HD], keys[:, cols], (((1,), (1,)), ((), ())),
                preferred_element_type=jnp.float32,
            )
            w = jnp.exp2(jnp.tanh(s * (HD ** (-0.5) / soft_cap)) * (soft_cap * LOG2E))
            if masked:
                keep = lax.broadcasted_iota(jnp.int32, w.shape, 0) >= lax.broadcasted_iota(
                    jnp.int32, w.shape, 1
                )
                w = jnp.where(keep, w, 0.0)
            folded = w[:, :128]
            for i in range(1, w.shape[1] // 128):
                folded = folded + w[:, i * 128 : (i + 1) * 128]
            o = jnp.dot(w.astype(jnp.bfloat16), values[:, cols], preferred_element_type=jnp.float32)
            if masked:
                den[h] = folded
                acc[h] = o
            else:
                den[h] += folded
                acc[h] += o

    stages = ((kbuf, kstage, kgot), (vbuf, vstage, vgot))

    def cache_copy(h, to, slot):
        return pltpu.make_async_remote_copy(
            src_ref=stages[h][1].at[to], dst_ref=stages[h][2].at[slot],
            send_sem=cache_send.at[to, h], recv_sem=cache_recv.at[slot, h],
            device_id={"seq": to}, device_id_type=MESH,
        )

    def select(buf, origin, chosen):
        got = jnp.zeros(chosen.shape, jnp.float32)
        for b in range(n):
            rows = buf[origin, b * block_rows : (b + 1) * block_rows, :]
            got = jnp.where(chosen == b, rows.astype(jnp.float32), got)
        return got.astype(jnp.bfloat16)

    def owned(device):
        block = own_ref[0, 0] * 0
        for b in range(n):
            block = block + jnp.where(own_ref[0, b] == device, b, 0)
        return jnp.full((block_rows, kv_width), block, jnp.int32)

    def stage(to, carry):
        chosen = owned(to)
        for buf, staged, _ in stages:
            staged[to] = select(buf, me, chosen)
        return carry

    lax.fori_loop(0, me, stage, 0)
    attend(kbuf.at[me], vbuf.at[me], True)

    def post(to, carry):
        for h in (0, 1):
            cache_copy(h, to, me).start()
        return carry

    lax.fori_loop(0, me, post, 0)

    def phase(d, carry):
        e = d - 1
        for h in (0, 1):
            pl.when(z - d >= 0)(functools.partial(handle, z - d, y, h))
        for h in (1, 0):
            there = (z - e >= 0) & ((e > 0) | (y == 1))
            pl.when(there)(functools.partial(handle, z - e, 1 - y, h))

        def one(i, carry):
            zz = z - d + i
            origin = zz * 2 + jnp.where(i == 0, y, 1 - y)

            @pl.when((zz >= 0) & (origin < me))
            def _():
                attend(kbuf.at[origin], vbuf.at[origin], False)

            return carry

        lax.fori_loop(0, 2, one, 0)
        return carry

    lax.fori_loop(1, nz + 1, phase, 0)

    for h in range(heads):
        att[:, h * HD : (h + 1) * HD] = (
            acc[h] / jnp.sum(den[h], axis=-1, keepdims=True)
        ).astype(jnp.bfloat16)

    chunks = shard // ROWS

    def rs_copy(kind, r, src, dst, to):
        return pltpu.make_async_remote_copy(
            src_ref=src.at[r], dst_ref=dst.at[r], send_sem=rs_send.at[kind, r],
            recv_sem=rs_recv.at[kind, r], device_id={"tp": to}, device_id_type=MESH,
        )

    def sib_copy(r):
        return rs_copy(0, r, to_sib, from_sib, sib)

    def x_copy(r):
        return rs_copy(1, r, to_x, from_x, across)

    def sib2_copy(r):
        return rs_copy(2, r, to_sib2, from_sib2, sib)

    def part(f, r):
        rows = att[pl.ds(pl.multiple_of(r * ROWS, ROWS), ROWS), :]
        return jnp.dot(rows, wbuf[f], preferred_element_type=jnp.float32)

    for f in range(4):
        w_copy(f).wait()

    def first(r, carry):
        to_sib[r] = part(diagonal, r).astype(jnp.bfloat16)
        sib_copy(r).start()
        return carry

    def second(r, carry):
        mine = part(across, r)
        sib_copy(r).wait_recv()
        to_x[r] = (mine + from_sib[r].astype(jnp.float32)).astype(jnp.bfloat16)
        x_copy(r).start()
        return carry

    def third(r, carry):
        to_sib2[r] = part(sib, r).astype(jnp.bfloat16)
        sib2_copy(r).start()
        return carry

    def fourth(r, carry):
        total[r] = part(t, r)
        return carry

    for step in (first, second, third, fourth):
        lax.fori_loop(0, chunks, step, 0)

    chosen = owned(me)
    local_row = lax.broadcasted_iota(jnp.int32, chosen.shape, 0)
    bound = jnp.full(chosen.shape, len_ref[0], jnp.int32)

    def cache(origin, carry):
        pos = local_row + chosen * block_rows + origin * shard
        live = (pos < bound) & (pos >= bound - WINDOW)
        start_row = pl.multiple_of(origin * block_rows, block_rows)

        @pl.when(origin <= me)
        def _():
            spot = jnp.where(live, chosen, -1)
            for (buf, _, _), out in zip(stages, (ck_ref, cv_ref)):
                out[pl.ds(start_row, block_rows), :] = select(buf, origin, spot)

        @pl.when(origin > me)
        def _():
            for h, out in enumerate((ck_ref, cv_ref)):
                cache_copy(h, origin, origin).wait_recv()
                got = stages[h][2][origin].astype(jnp.float32)
                out[pl.ds(start_row, block_rows), :] = jnp.where(live, got, 0.0).astype(
                    jnp.bfloat16
                )

        return carry

    lax.fori_loop(0, n, cache, 0)
    rest = ck_ref.shape[0] - n * block_rows
    if rest:
        for out in (ck_ref, cv_ref):
            out[n * block_rows :, :] = jnp.zeros((rest, kv_width), jnp.bfloat16)
    outs = [
        pltpu.make_async_copy(src, dst, out_sem.at[i])
        for i, (src, dst) in enumerate(((ck_ref, ck_hbm), (cv_ref, cv_hbm), (hid_ref, hid_hbm)))
    ]
    outs[0].start()
    outs[1].start()

    for r in range(chunks):
        sib2_copy(r).wait_recv()
        x_copy(r).wait_recv()
        branch = total[r] + from_sib2[r].astype(jnp.float32) + from_x[r].astype(jnp.float32)
        total[r] = branch
        squared = branch * branch
        folded = squared[:, :128]
        for i in range(1, squared.shape[1] // 128):
            folded = folded + squared[:, i * 128 : (i + 1) * 128]
        line = jnp.sum(folded.T, axis=0, keepdims=True)
        sq_out[:, r * ROWS : (r + 1) * ROWS] = jnp.broadcast_to(line, (8, ROWS))

    def sq_copy(i, to, slot):
        return pltpu.make_async_remote_copy(
            src_ref=sq_out, dst_ref=sq_in.at[slot], send_sem=sq_send.at[i],
            recv_sem=sq_recv.at[slot], device_id={"tp": to}, device_id_type=MESH,
        )

    peers = (sib, across, diagonal)
    for i, peer in enumerate(peers):
        sq_copy(i, peer, t).start()
    squares = sq_out[...]
    for i, peer in enumerate(peers):
        sq_copy(i, peer, peer).wait_recv()
        squares = squares + sq_in[peer]
    loads[4].wait()
    loads[5].wait()
    factor = lax.rsqrt(squares / D + norm_eps)
    for r in range(chunks):
        line = jnp.broadcast_to(factor[:1, r * ROWS : (r + 1) * ROWS], (128, ROWS))
        spread = line.T
        for i in range(res_ref.shape[1] // 128):
            cols = slice(i * 128, (i + 1) * 128)
            rows = slice(r * ROWS, (r + 1) * ROWS)
            normed = total[r, :, cols] * spread * scale_ref[cols].reshape(1, 128)
            hid_ref[rows, cols] = (res_ref[rows, cols].astype(jnp.float32) + normed).astype(
                jnp.bfloat16
            )

    outs[2].start()
    for i, peer in enumerate(peers):
        sq_copy(i, peer, t).wait_send()
    for r in range(chunks):
        sib_copy(r).wait_send()
        x_copy(r).wait_send()
        sib2_copy(r).wait_send()

    def drain(origin, carry):
        for h in (0, 1):
            for go, copy in routes(origin // 2, origin % 2, h):
                pl.when(go)(copy.wait_send)
        return carry

    lax.fori_loop(0, me + 1, drain, 0)

    def settle(to, carry):
        for h in (0, 1):
            cache_copy(h, to, me).wait_send()
        return carry

    lax.fori_loop(0, me, settle, 0)
    for out in outs:
        out.wait()


def put_out(*refs):
    count = (len(refs) - 1) // 3
    sems = refs[-1]
    copies = [
        (
            pltpu.make_async_copy(refs[i], refs[2 * count + i], sems.at[0, i]),
            pltpu.make_async_copy(refs[2 * count + i], refs[count + i], sems.at[1, i]),
        )
        for i in range(count)
    ]
    for read, _ in copies:
        read.start()
    for read, write in copies:
        read.wait()
        write.start()
    for _, write in copies:
        write.wait()


def fused(n, queries, key_rows, value_rows, residual, out_weight, post_scale, lengths, owners):
    shard, q_width = queries.shape[1:]
    kv_width = key_rows.shape[2]
    width = residual.shape[2]
    heads = q_width // HD
    chunks = shard // ROWS
    cache_rows = WINDOW // n
    smem = pl.BlockSpec(memory_space=pltpu.SMEM)
    apart = pl.BlockSpec(memory_space=pl.ANY)
    owned_rows = pltpu.VMEM((n, shard // n, kv_width), jnp.bfloat16)
    half = pltpu.VMEM((chunks, ROWS, width), jnp.bfloat16)
    hidden, ck, cv = pl.pallas_call(
        functools.partial(layer_kernel, n),
        out_shape=(
            jax.ShapeDtypeStruct((shard, width), jnp.bfloat16),
            jax.ShapeDtypeStruct((cache_rows, kv_width), jnp.bfloat16),
            jax.ShapeDtypeStruct((cache_rows, kv_width), jnp.bfloat16),
        ),
        in_specs=[apart] * 5 + [smem] + [apart] * 2,
        out_specs=(apart,) * 3,
        scratch_shapes=[
            pltpu.VMEM((shard, width), jnp.bfloat16),
            pltpu.VMEM((cache_rows, kv_width), jnp.bfloat16),
            pltpu.VMEM((cache_rows, kv_width), jnp.bfloat16),
            pltpu.VMEM((shard, q_width), jnp.bfloat16),
            pltpu.VMEM((shard, width), jnp.bfloat16),
            pltpu.VMEM((width,), jnp.float32),
            pltpu.SMEM((1, n), jnp.int32),
            owned_rows, owned_rows, owned_rows, owned_rows,
            pltpu.VMEM((n, shard, kv_width), jnp.bfloat16),
            pltpu.VMEM((n, shard, kv_width), jnp.bfloat16),
            pltpu.VMEM((4, q_width, width), jnp.bfloat16),
            pltpu.VMEM((heads, shard, HD), jnp.float32),
            pltpu.VMEM((heads, shard, 128), jnp.float32),
            pltpu.VMEM((shard, q_width), jnp.bfloat16),
            half, half, half, half, half, half,
            pltpu.VMEM((chunks, ROWS, width), jnp.float32),
            pltpu.VMEM((8, shard), jnp.float32),
            pltpu.VMEM((4, 8, shard), jnp.float32),
            pltpu.SemaphoreType.DMA((6,)),
            pltpu.SemaphoreType.DMA((n, 2, 2)),
            pltpu.SemaphoreType.DMA((n, 2)),
            pltpu.SemaphoreType.DMA((4,)),
            pltpu.SemaphoreType.DMA((3, chunks)),
            pltpu.SemaphoreType.DMA((3, chunks)),
            pltpu.SemaphoreType.DMA((3,)),
            pltpu.SemaphoreType.DMA((4,)),
            pltpu.SemaphoreType.DMA((n, 2)),
            pltpu.SemaphoreType.DMA((n, 2)),
            pltpu.SemaphoreType.DMA((3,)),
        ],
        compiler_params=pltpu.CompilerParams(
            collective_id=0, has_side_effects=True, vmem_limit_bytes=60 * 1024 * 1024
        ),
    )(
        queries[0], key_rows[0], value_rows[0], residual[0], post_scale, lengths, owners,
        out_weight,
    )
    made = (hidden, ck, cv)
    hidden, ck, cv = pl.pallas_call(
        put_out,
        out_shape=tuple(jax.ShapeDtypeStruct(a.shape, a.dtype) for a in made),
        in_specs=[apart] * len(made),
        out_specs=(apart,) * len(made),
        scratch_shapes=[pltpu.VMEM(a.shape, a.dtype) for a in made]
        + [pltpu.SemaphoreType.DMA((2, len(made)))],
    )(*made)
    return hidden[None], ck[None], cv[None]


def solution(mesh):
    placed = (
        P(None, "seq", "tp"),
        P(None, "seq", "tp"),
        P(None, "seq", "tp"),
        P(None, "seq", "tp"),
        P("tp", None),
        P("tp"),
        P(),
        P(),
    )
    return jax.shard_map(
        local,
        mesh=mesh,
        in_specs=placed,
        out_specs=(P(None, "seq", "tp"), P(None, "seq", "tp"), P(None, "seq", "tp")),
        check_vma=False,
    )
```

profile of v0, /device:TPU:25, one launch (start us, length us, event | category | flops | bytes accessed | tf_op | source)
XLA Modules:
  0.0 67.3 jit_solution(12502396550537452660)
XLA Ops:
  1.3 63.8 %shard_map.103 = (bf16[256,896]{1,0:T(8,128)(2,1)}, bf16[512,512]{1,0:T(8,128)(2,1)}, bf16[512,512]{1,0:T(8,128)(2,1)}) custom-call(bf16[256,1024]{1,0:T(8,128)(2,1)} %bitcast.7, bf16[256,512]{1,0:T(8,128)(2,1)} %bitcast.9, bf16[256,512]{1,0:T(8,128)(2,1)} %bitcast.10, bf16[256,896]{1,0:T(8,128)(2,1)} %bitcast.8, f32[896]{0:T(1024)} %scale_hbm.1, ...), custom_call_target="tpu_custom_call" | custom-call | tf_op jit(solution)/shard_map/pallas_call | solution.py:502
  65.1 2.2 %shard_map.104 = (bf16[256,896]{1,0:T(8,128)(2,1)}, bf16[512,512]{1,0:T(8,128)(2,1)}, bf16[512,512]{1,0:T(8,128)(2,1)}) custom-call(bf16[256,896]{1,0:T(8,128)(2,1)} %get-tuple-element.9.refs_0_, bf16[512,512]{1,0:T(8,128)(2,1)} %get-tuple-element.10.refs_1_, bf16[512,512]{1,0:T(8,128)(2,1)} %get-tuple-element.11.refs_2_), custom_call_target="tpu_custom_call" | custom-call | tf_op jit(solution)/shard_map/pallas_call | solution.py:550
where the time goes:
time: 67.4 us; the launch traced here: 67.3 us
  Pallas kernels  66 us (98%)
  between operations  1.29 us (2%)
    pallas_call x1, Pallas kernels, fused(): pl.pallas_call(functools.partial(layer_kernel, n), out_shape=(jax.ShapeDt...  63.8 us
    pallas_call x1, Pallas kernels, fused(): pl.pallas_call(put_out, out_shape=tuple((jax.ShapeDtypeStruct(a.shape, a....  2.2 us

commit v1 on v0

--- a/solution.py
+++ b/solution.py
@@ -55,8 +55,8 @@
     seq_count, shard_len, query_width = queries.shape
     seq_size = lax.axis_size("seq")
     if (
-        seq_count == 1 and lax.axis_size("tp") == 4 and seq_size % 2 == 0
-        and seq_size * shard_len <= WINDOW
+        seq_count == 1 and lax.axis_size("tp") == 4 and seq_size % 2 == 0 and seq_size >= 4
+        and seq_size * shard_len <= WINDOW and key_rows.shape[2] == 2 * HD
     ):
         return fused(
             seq_size, queries, key_rows, value_rows, residual, out_weight, post_scale, lengths,
@@ -147,12 +147,16 @@
 def layer_kernel(
     n, q_hbm, k_hbm, v_hbm, res_hbm, scale_hbm, len_ref, own_hbm, w_ref,
     hid_hbm, ck_hbm, cv_hbm,
-    hid_ref, ck_ref, cv_ref, q_ref, res_ref, scale_ref, own_ref, kstage, vstage, kgot, vgot,
-    kbuf, vbuf, wbuf, acc, den, att, to_sib, to_x, to_sib2, from_sib, from_x, from_sib2,
-    total, sq_out, sq_in,
-    in_sem, send_sem, recv_sem, w_sem, rs_send, rs_recv, sq_send, sq_recv, cache_send, cache_recv, out_sem,
+    hid_ref, ck_ref, cv_ref, qall, qpart, res_ref, scale_ref, own_ref, kv, other,
+    down_out, down_in, pair_out, pair_in, line_out, line_in, skew_out,
+    wbuf, acc, den, att, att_out, num_out, num_in, den_out, den_in,
+    to_sib, to_x, to_sib2, from_sib, from_x, from_sib2, total, sq_out, sq_in,
+    in_sem, w_sem, y_send, y_recv, z_send, z_recv, q_send, q_recv, num_send, num_recv, den_send, den_recv,
+    down_send, down_recv, pair_send, pair_recv, line_send, line_recv, skew_send, att_send, att_recv,
+    rs_send, rs_recv, sq_send, sq_recv, out_sem,
 ):
     nz = n // 2
+    top = nz - 1
     me = lax.axis_index("seq")
     t = lax.axis_index("tp")
     z, y = me // 2, me % 2
@@ -160,30 +164,35 @@
     sib = x * 2 + (1 - c)
     across = (1 - x) * 2 + c
     diagonal = (1 - x) * 2 + (1 - c)
-    shard = q_ref.shape[0]
-    heads = q_ref.shape[1] // HD
-    kv_width = k_hbm.shape[1]
-    group = q_ref.shape[1] // kv_width
+    partner = z * 2 + (1 - y)
+    shard = kv.shape[2]
+    width = res_ref.shape[1]
+    group_cols = qpart.shape[1]
+    group = group_cols // HD
     block_rows = shard // n
-    bufs = (kbuf, vbuf)
+    chunks = shard // ROWS
+    lends = (c == 1) & (z == top)
+    hosts = (c == 1) & (z == top - 1)
+    takes_kv = (z < top) | (c == 0)
+    sends_kv = (z < top - 1) | ((z < top) & (c == 0))
+
+    def half(ref, which, cols):
+        return ref.at[:, pl.ds(pl.multiple_of(which * cols, cols), cols)]
+
     loads = [
         pltpu.make_async_copy(src, dst, in_sem.at[i])
         for i, (src, dst) in enumerate(
             (
-                (k_hbm, kbuf.at[me]), (v_hbm, vbuf.at[me]), (q_hbm, q_ref), (own_hbm, own_ref),
-                (res_hbm, res_ref), (scale_hbm, scale_ref),
+                (half(k_hbm, 1 - y, HD), other.at[0]), (half(v_hbm, 1 - y, HD), other.at[1]),
+                (half(k_hbm, y, HD), kv.at[me, 0]), (half(v_hbm, y, HD), kv.at[me, 1]),
+                (half(q_hbm, 1 - y, group_cols), qpart), (half(q_hbm, y, group_cols), qall.at[y]),
+                (own_hbm, own_ref), (res_hbm, res_ref), (scale_hbm, scale_ref),
             )
         )
     ]
-    for load in loads:
+    for load in loads[:7]:
         load.start()
 
-    def w_copy(f):
-        return pltpu.make_async_copy(
-            w_ref.at[:, pl.ds(f * res_ref.shape[1], res_ref.shape[1])], wbuf.at[f], w_sem.at[f]
-        )
-
-    partner = z * 2 + (1 - y)
     barrier = pltpu.get_barrier_semaphore()
     for peer in (sib, across, diagonal):
         pl.semaphore_signal(barrier, inc=1, device_id={"tp": peer}, device_id_type=MESH)
@@ -191,51 +200,134 @@
         pl.semaphore_signal(
             barrier, inc=1, device_id={"seq": lax.rem(me + hop, n)}, device_id_type=MESH
         )
+
+    def clear(s, carry):
+        acc[s] = jnp.zeros(acc.shape[1:], jnp.float32)
+        den[s] = jnp.zeros(den.shape[1:], jnp.float32)
+        return carry
+
+    lax.fori_loop(0, acc.shape[0], clear, 0)
     pl.semaphore_wait(barrier, n + 2)
 
-    def routes(zo, yo, h):
-        special = ((zo == 0) & (yo == 0)) if h == 1 else False
-        line = (yo == y) | special
-        crossing = (yo == y) & (zo + y <= z) & ((zo == z) | jnp.logical_not(special))
-        origin = zo * 2 + yo
-        plan = ((line & (zo <= z) & (z < nz - 1), me + 2), (crossing, partner))
-        out = []
-        for way, (go, to) in enumerate(plan):
-            copy = pltpu.make_async_remote_copy(
-                src_ref=bufs[h].at[origin],
-                dst_ref=bufs[h].at[origin],
-                send_sem=send_sem.at[origin, h, way],
-                recv_sem=recv_sem.at[origin, h],
-                device_id={"seq": to},
-                device_id_type=MESH,
-            )
-            out.append((go, copy))
-        return out
-
-    def start(zo, yo, h):
-        for go, copy in routes(zo, yo, h):
-            pl.when(go)(copy.start)
-
-    def handle(zo, yo, h):
-        routes(zo, yo, h)[0][1].wait_recv()
-        start(zo, yo, h)
+    def remote(src, dst, send, recv, to):
+        return pltpu.make_async_remote_copy(
+            src_ref=src, dst_ref=dst, send_sem=send, recv_sem=recv, device_id=to,
+            device_id_type=MESH,
+        )
+
+    def y_copy(h, origin):
+        return remote(
+            other.at[h], kv.at[origin, h], y_send.at[h], y_recv.at[h], {"seq": partner}
+        )
+
+    def yq_copy(slot):
+        return remote(qpart, qall.at[slot], y_send.at[2], y_recv.at[2], {"seq": partner})
+
+    def z_copy(origin, h):
+        return remote(
+            kv.at[origin, h], kv.at[origin, h], z_send.at[origin, h], z_recv.at[origin, h],
+            {"seq": me + 2},
+        )
+
+    def lend_copy(yq):
+        return remote(
+            qall.at[yq], qall.at[2 + yq], q_send.at[yq], q_recv.at[yq], {"seq": me - 2}
+        )
+
+    def w_copy(f):
+        return pltpu.make_async_copy(
+            w_ref.at[:, pl.ds(f * width, width)], wbuf.at[f], w_sem.at[f]
+        )
 
     for h in (0, 1):
-        loads[h].wait()
-        start(z, y, h)
+        loads[2 + h].wait()
+        pl.when(sends_kv)(z_copy(me, h).start)
+    for load in (loads[0], loads[1], loads[4], loads[5]):
+        load.wait()
+
+    @pl.when(z == top)
+    def _():
+        yq_copy(y).start()
+        for h in (0, 1):
+            y_copy(h, me).start()
+
+    @pl.when(z < top)
+    def _():
+        for h in (0, 1):
+            y_copy(h, me).start()
+        yq_copy(y).start()
+
+    pl.when(lends)(lend_copy(y).start)
+    loads[6].wait()
     for f in range(4):
         w_copy(f).start()
-    loads[2].wait()
-    loads[3].wait()
-
-    def attend(keys, values, masked):
-        for h in range(heads):
-            cols = pl.ds((h // group) * HD, HD)
-            s = lax.dot_general(
-                q_ref[:, h * HD : (h + 1) * HD], keys[:, cols], (((1,), (1,)), ((), ())),
+    for load in loads[7:]:
+        load.start()
+
+    def owned(device):
+        block = own_ref[0, 0] * 0
+        for b in range(n):
+            block = block + jnp.where(own_ref[0, b] == device, b, 0)
+        return jnp.full((block_rows, HD), block, jnp.int32)
+
+    def select(ref, lead, chosen):
+        got = jnp.zeros(chosen.shape, jnp.float32)
+        for b in range(n):
+            rows = ref[(*lead, slice(b * block_rows, (b + 1) * block_rows))]
+            got = jnp.where(chosen == b, rows.astype(jnp.float32), got)
+        return got.astype(jnp.bfloat16)
+
+    def down_copy(to, slot):
+        return remote(
+            down_out.at[to], down_in.at[slot], down_send.at[to], down_recv.at[slot], {"seq": to}
+        )
+
+    def stage(to, carry):
+        chosen = owned(to)
+        for h in (0, 1):
+            down_out[to, h, y] = select(kv, (me, h), chosen)
+            down_out[to, h, 1 - y] = select(other, (h,), chosen)
+        return carry
+
+    def post(to, carry):
+        down_copy(to, me).start()
+        return carry
+
+    lax.fori_loop(0, 2 * z, stage, 0)
+
+    @pl.when(lends)
+    def _():
+        yq_copy(1 - y).wait_recv()
+        lend_copy(1 - y).start()
+
+    for h in (0, 1):
+        y_copy(h, partner).wait_recv()
+        pl.when(sends_kv)(z_copy(partner, h).start)
+    lax.fori_loop(0, 2 * z, post, 0)
+
+    def take(d, j):
+        origin = 2 * (z - d) + jnp.where(j == 0, y, 1 - y)
+        for h in (0, 1):
+            z_copy(origin, h).wait_recv()
+            pl.when(sends_kv)(z_copy(origin, h).start)
+
+    @pl.when((z > 0) & takes_kv)
+    def _():
+        take(1, 0)
+        take(1, 1)
+
+    @pl.when(jnp.logical_not(lends))
+    def _():
+        yq_copy(1 - y).wait_recv()
+
+    def attend(s, origin, masked):
+        for hh in range(group):
+            slot = s * group + hh
+            scores = lax.dot_general(
+                qall[s, :, hh * HD : (hh + 1) * HD], kv[origin, 0], (((1,), (1,)), ((), ())),
                 preferred_element_type=jnp.float32,
             )
-            w = jnp.exp2(jnp.tanh(s * (HD ** (-0.5) / soft_cap)) * (soft_cap * LOG2E))
+            w = jnp.exp2(jnp.tanh(scores * (HD ** (-0.5) / soft_cap)) * (soft_cap * LOG2E))
             if masked:
                 keep = lax.broadcasted_iota(jnp.int32, w.shape, 0) >= lax.broadcasted_iota(
                     jnp.int32, w.shape, 1
@@ -244,86 +336,177 @@
             folded = w[:, :128]
             for i in range(1, w.shape[1] // 128):
                 folded = folded + w[:, i * 128 : (i + 1) * 128]
-            o = jnp.dot(w.astype(jnp.bfloat16), values[:, cols], preferred_element_type=jnp.float32)
-            if masked:
-                den[h] = folded
-                acc[h] = o
-            else:
-                den[h] += folded
-                acc[h] += o
-
-    stages = ((kbuf, kstage, kgot), (vbuf, vstage, vgot))
-
-    def cache_copy(h, to, slot):
-        return pltpu.make_async_remote_copy(
-            src_ref=stages[h][1].at[to], dst_ref=stages[h][2].at[slot],
-            send_sem=cache_send.at[to, h], recv_sem=cache_recv.at[slot, h],
-            device_id={"seq": to}, device_id_type=MESH,
-        )
-
-    def select(buf, origin, chosen):
-        got = jnp.zeros(chosen.shape, jnp.float32)
-        for b in range(n):
-            rows = buf[origin, b * block_rows : (b + 1) * block_rows, :]
-            got = jnp.where(chosen == b, rows.astype(jnp.float32), got)
-        return got.astype(jnp.bfloat16)
-
-    def owned(device):
-        block = own_ref[0, 0] * 0
-        for b in range(n):
-            block = block + jnp.where(own_ref[0, b] == device, b, 0)
-        return jnp.full((block_rows, kv_width), block, jnp.int32)
-
-    def stage(to, carry):
-        chosen = owned(to)
-        for buf, staged, _ in stages:
-            staged[to] = select(buf, me, chosen)
-        return carry
-
-    lax.fori_loop(0, me, stage, 0)
-    attend(kbuf.at[me], vbuf.at[me], True)
-
-    def post(to, carry):
-        for h in (0, 1):
-            cache_copy(h, to, me).start()
-        return carry
-
-    lax.fori_loop(0, me, post, 0)
+            den[slot] += folded
+            acc[slot] += jnp.dot(
+                w.astype(jnp.bfloat16), kv[origin, 1], preferred_element_type=jnp.float32
+            )
+
+    def diagonal_block(s, carry):
+        attend(s, 2 * z + s, True)
+        return carry
+
+    lax.fori_loop(0, 2, diagonal_block, 0)
+    attend(1, 2 * z, False)
+
+    @pl.when(hosts)
+    def _():
+        for yq in (0, 1):
+            lend_copy(yq).wait_recv()
+
+        def one(i, carry):
+            attend(2 + i // 2, 2 * z + i % 2, False)
+            return carry
+
+        lax.fori_loop(0, 4, one, 0)
+
+    def pair_copy(zo):
+        return remote(
+            pair_out.at[zo], pair_in.at[zo], pair_send.at[zo], pair_recv.at[zo], {"seq": partner}
+        )
+
+    def line_copy(zo):
+        return remote(
+            line_out.at[zo], line_in.at[zo], line_send.at[zo], line_recv.at[zo], {"seq": me + 2}
+        )
+
+    def skew_copy(zo):
+        return remote(
+            skew_out.at[zo], pair_in.at[zo], skew_send.at[zo], pair_recv.at[zo],
+            {"seq": partner + 2},
+        )
+
+    def gather(zo, device, out):
+        chosen = owned(device)
+        for yo in (0, 1):
+            for h in (0, 1):
+                out[zo, yo, h] = select(kv, (2 * zo + yo, h), chosen)
+
+    def pass_cache(zo):
+        @pl.when((zo == z) | takes_kv)
+        def _():
+            gather(zo, partner, pair_out)
+            pair_copy(zo).start()
+
+        @pl.when(hosts)
+        def _():
+            gather(zo, me + 2, line_out)
+            line_copy(zo).start()
+            gather(zo, partner + 2, skew_out)
+            skew_copy(zo).start()
+
+    slots = jnp.where(hosts, 4, 2)
 
     def phase(d, carry):
-        e = d - 1
-        for h in (0, 1):
-            pl.when(z - d >= 0)(functools.partial(handle, z - d, y, h))
-        for h in (1, 0):
-            there = (z - e >= 0) & ((e > 0) | (y == 1))
-            pl.when(there)(functools.partial(handle, z - e, 1 - y, h))
-
-        def one(i, carry):
-            zz = z - d + i
-            origin = zz * 2 + jnp.where(i == 0, y, 1 - y)
-
-            @pl.when((zz >= 0) & (origin < me))
+        @pl.when(z - d + 1 >= 1)
+        def _():
+            pass_cache(z - d + 1)
+
+        def side(j, carry):
+            @pl.when((z - d >= 0) & takes_kv)
             def _():
-                attend(kbuf.at[origin], vbuf.at[origin], False)
+                @pl.when(d > 1)
+                def _():
+                    take(d, j)
+
+                origin = 2 * (z - d) + jnp.where(j == 0, y, 1 - y)
+
+                def one(s, carry):
+                    attend(s, origin, False)
+                    return carry
+
+                lax.fori_loop(0, slots, one, 0)
 
             return carry
 
-        lax.fori_loop(0, 2, one, 0)
-        return carry
-
-    lax.fori_loop(1, nz + 1, phase, 0)
-
-    for h in range(heads):
-        att[:, h * HD : (h + 1) * HD] = (
-            acc[h] / jnp.sum(den[h], axis=-1, keepdims=True)
-        ).astype(jnp.bfloat16)
-
-    chunks = shard // ROWS
+        lax.fori_loop(0, 2, side, 0)
+        return carry
+
+    lax.fori_loop(1, nz, phase, 0)
+
+    def num_copy(yq, r):
+        return remote(
+            num_out.at[yq, r], num_in.at[yq, r], num_send.at[yq, r], num_recv.at[yq, r],
+            {"seq": me + 2},
+        )
+
+    def den_copy():
+        return remote(den_out, den_in, den_send.at[0], den_recv.at[0], {"seq": me + 2})
+
+    def rows_of(r):
+        return pl.ds(pl.multiple_of(r * ROWS, ROWS), ROWS)
+
+    @pl.when(hosts)
+    def _():
+        for s in range(2 * group):
+            for r in range(chunks):
+                cols = slice(r * ROWS, (r + 1) * ROWS)
+                line = jnp.sum(den[2 * group + s, cols, :].T, axis=0, keepdims=True)
+                den_out[s, :, cols] = jnp.broadcast_to(line, (8, ROWS))
+        den_copy().start()
+
+        def give(i, carry):
+            yq = jnp.where(i < chunks, 1 - y, y)
+            r = i % chunks
+            for hh in range(group):
+                num_out[yq, r, :, hh * HD : (hh + 1) * HD] = acc[
+                    (2 + yq) * group + hh, rows_of(r), :
+                ].astype(jnp.bfloat16)
+            num_copy(yq, r).start()
+            return carry
+
+        lax.fori_loop(0, 2 * chunks, give, 0)
+
+    def att_copy(r, g):
+        return remote(
+            att_out.at[r], att.at[g, r], att_send.at[r], att_recv.at[r], {"seq": partner}
+        )
+
+    pl.when(lends)(den_copy().wait_recv)
+
+    def finish(yq, r, put):
+        rows = rows_of(r)
+
+        @pl.when(lends)
+        def _():
+            num_copy(yq, r).wait_recv()
+            for hh in range(group):
+                slot = yq * group + hh
+                acc[slot, rows, :] += num_in[yq, r, :, hh * HD : (hh + 1) * HD].astype(jnp.float32)
+                line = den_in[slot, :1, rows]
+                spread = jnp.broadcast_to(line, (128, ROWS)).T
+                first = lax.broadcasted_iota(jnp.int32, spread.shape, 1) == 0
+                den[slot, rows, :] += jnp.where(first, spread, 0.0)
+
+        for hh in range(group):
+            slot = yq * group + hh
+            put(
+                hh,
+                (
+                    acc[slot, rows, :] / jnp.sum(den[slot, rows, :], axis=-1, keepdims=True)
+                ).astype(jnp.bfloat16),
+            )
+
+    def away(r, carry):
+        def put(hh, value):
+            att_out[r, :, hh * HD : (hh + 1) * HD] = value
+
+        finish(1 - y, r, put)
+        att_copy(r, y).start()
+        return carry
+
+    def home(r, carry):
+        def put(hh, value):
+            att[y, r, :, hh * HD : (hh + 1) * HD] = value
+
+        finish(y, r, put)
+        return carry
+
+    lax.fori_loop(0, chunks, away, 0)
+    lax.fori_loop(0, chunks, home, 0)
 
     def rs_copy(kind, r, src, dst, to):
-        return pltpu.make_async_remote_copy(
-            src_ref=src.at[r], dst_ref=dst.at[r], send_sem=rs_send.at[kind, r],
-            recv_sem=rs_recv.at[kind, r], device_id={"tp": to}, device_id_type=MESH,
+        return remote(
+            src.at[r], dst.at[r], rs_send.at[kind, r], rs_recv.at[kind, r], {"tp": to}
         )
 
     def sib_copy(r):
@@ -336,13 +519,15 @@
         return rs_copy(2, r, to_sib2, from_sib2, sib)
 
     def part(f, r):
-        rows = att[pl.ds(pl.multiple_of(r * ROWS, ROWS), ROWS), :]
-        return jnp.dot(rows, wbuf[f], preferred_element_type=jnp.float32)
+        return jnp.dot(
+            att[0, r], wbuf[f, :group_cols, :], preferred_element_type=jnp.float32
+        ) + jnp.dot(att[1, r], wbuf[f, group_cols:, :], preferred_element_type=jnp.float32)
 
     for f in range(4):
         w_copy(f).wait()
 
     def first(r, carry):
+        att_copy(r, 1 - y).wait_recv()
         to_sib[r] = part(diagonal, r).astype(jnp.bfloat16)
         sib_copy(r).start()
         return carry
@@ -363,40 +548,71 @@
         total[r] = part(t, r)
         return carry
 
-    for step in (first, second, third, fourth):
+    for step in (first, second):
         lax.fori_loop(0, chunks, step, 0)
 
-    chosen = owned(me)
-    local_row = lax.broadcasted_iota(jnp.int32, chosen.shape, 0)
-    bound = jnp.full(chosen.shape, len_ref[0], jnp.int32)
-
-    def cache(origin, carry):
-        pos = local_row + chosen * block_rows + origin * shard
-        live = (pos < bound) & (pos >= bound - WINDOW)
-        start_row = pl.multiple_of(origin * block_rows, block_rows)
-
-        @pl.when(origin <= me)
+    pass_cache(0)
+
+    for step in (third, fourth):
+        lax.fori_loop(0, chunks, step, 0)
+
+    mine_blocks = owned(me)
+    local_row = lax.broadcasted_iota(jnp.int32, mine_blocks.shape, 0)
+    bound = jnp.full(mine_blocks.shape, len_ref[0], jnp.int32)
+
+    def cache(zo, carry):
+        far = lends & (zo < top)
+
+        @pl.when(zo <= z)
         def _():
-            spot = jnp.where(live, chosen, -1)
-            for (buf, _, _), out in zip(stages, (ck_ref, cv_ref)):
-                out[pl.ds(start_row, block_rows), :] = select(buf, origin, spot)
-
-        @pl.when(origin > me)
+            skew_copy(zo).wait_recv()
+
+        @pl.when(far)
         def _():
+            line_copy(zo).wait_recv()
+
+        for yo in (0, 1):
+            origin = 2 * zo + yo
+            pos = local_row + mine_blocks * block_rows + origin * shard
+            live = (pos < bound) & (pos >= bound - WINDOW)
+            rows = pl.ds(pl.multiple_of(origin * block_rows, block_rows), block_rows)
+
+            @pl.when(zo > z)
+            def _():
+                down_copy(origin, origin).wait_recv()
+
             for h, out in enumerate((ck_ref, cv_ref)):
-                cache_copy(h, origin, origin).wait_recv()
-                got = stages[h][2][origin].astype(jnp.float32)
-                out[pl.ds(start_row, block_rows), :] = jnp.where(live, got, 0.0).astype(
-                    jnp.bfloat16
-                )
-
-        return carry
-
-    lax.fori_loop(0, n, cache, 0)
+
+                def put(g, value):
+                    cols = pl.ds(pl.multiple_of(g * HD, HD), HD)
+                    out[rows, cols] = jnp.where(live, value.astype(jnp.float32), 0.0).astype(
+                        jnp.bfloat16
+                    )
+
+                @pl.when(zo > z)
+                def _():
+                    for g in (0, 1):
+                        put(g, down_in[origin, h, g])
+
+                @pl.when(zo <= z)
+                def _():
+                    put(1 - y, pair_in[zo, yo, h])
+
+                @pl.when((zo <= z) & jnp.logical_not(far))
+                def _():
+                    put(y, select(kv, (origin, h), mine_blocks))
+
+                @pl.when(far)
+                def _():
+                    put(y, line_in[zo, yo, h])
+
+        return carry
+
+    lax.fori_loop(0, nz, cache, 0)
     rest = ck_ref.shape[0] - n * block_rows
     if rest:
         for out in (ck_ref, cv_ref):
-            out[n * block_rows :, :] = jnp.zeros((rest, kv_width), jnp.bfloat16)
+            out[n * block_rows :, :] = jnp.zeros((rest, 2 * HD), jnp.bfloat16)
     outs = [
         pltpu.make_async_copy(src, dst, out_sem.at[i])
         for i, (src, dst) in enumerate(((ck_ref, ck_hbm), (cv_ref, cv_hbm), (hid_ref, hid_hbm)))
@@ -429,8 +645,8 @@
     for i, peer in enumerate(peers):
         sq_copy(i, peer, peer).wait_recv()
         squares = squares + sq_in[peer]
-    loads[4].wait()
-    loads[5].wait()
+    loads[7].wait()
+    loads[8].wait()
     factor = lax.rsqrt(squares / D + norm_eps)
     for r in range(chunks):
         line = jnp.broadcast_to(factor[:1, r * ROWS : (r + 1) * ROWS], (128, ROWS))
@@ -451,20 +667,52 @@
         x_copy(r).wait_send()
         sib2_copy(r).wait_send()
 
-    def drain(origin, carry):
+    for h in (0, 1):
+        y_copy(h, me).wait_send()
+    yq_copy(y).wait_send()
+    for r in range(chunks):
+        att_copy(r, y).wait_send()
+
+    def settle_kv(origin, carry):
         for h in (0, 1):
-            for go, copy in routes(origin // 2, origin % 2, h):
-                pl.when(go)(copy.wait_send)
-        return carry
-
-    lax.fori_loop(0, me + 1, drain, 0)
+            z_copy(origin, h).wait_send()
+        return carry
+
+    @pl.when(sends_kv)
+    def _():
+        lax.fori_loop(0, 2 * z + 2, settle_kv, 0)
+
+    @pl.when(lends)
+    def _():
+        for yq in (0, 1):
+            lend_copy(yq).wait_send()
+
+    @pl.when(hosts)
+    def _():
+        den_copy().wait_send()
+        for yq in (0, 1):
+            for r in range(chunks):
+                num_copy(yq, r).wait_send()
 
     def settle(to, carry):
-        for h in (0, 1):
-            cache_copy(h, to, me).wait_send()
-        return carry
-
-    lax.fori_loop(0, me, settle, 0)
+        down_copy(to, me).wait_send()
+        return carry
+
+    lax.fori_loop(0, 2 * z, settle, 0)
+
+    def settle_cache(zo, carry):
+        @pl.when((zo == z) | takes_kv)
+        def _():
+            pair_copy(zo).wait_send()
+
+        @pl.when(hosts)
+        def _():
+            line_copy(zo).wait_send()
+            skew_copy(zo).wait_send()
+
+        return carry
+
+    lax.fori_loop(0, z + 1, settle_cache, 0)
     for out in outs:
         out.wait()
 
@@ -497,7 +745,8 @@
     cache_rows = WINDOW // n
     smem = pl.BlockSpec(memory_space=pltpu.SMEM)
     apart = pl.BlockSpec(memory_space=pl.ANY)
-    owned_rows = pltpu.VMEM((n, shard // n, kv_width), jnp.bfloat16)
+    group_cols = q_width * HD // kv_width
+    slab = pltpu.VMEM((n // 2, 2, 2, shard // n, HD), jnp.bfloat16)
     half = pltpu.VMEM((chunks, ROWS, width), jnp.bfloat16)
     hidden, ck, cv = pl.pallas_call(
         functools.partial(layer_kernel, n),
@@ -512,31 +761,54 @@
             pltpu.VMEM((shard, width), jnp.bfloat16),
             pltpu.VMEM((cache_rows, kv_width), jnp.bfloat16),
             pltpu.VMEM((cache_rows, kv_width), jnp.bfloat16),
-            pltpu.VMEM((shard, q_width), jnp.bfloat16),
+            pltpu.VMEM((4, shard, group_cols), jnp.bfloat16),
+            pltpu.VMEM((shard, group_cols), jnp.bfloat16),
             pltpu.VMEM((shard, width), jnp.bfloat16),
             pltpu.VMEM((width,), jnp.float32),
             pltpu.SMEM((1, n), jnp.int32),
-            owned_rows, owned_rows, owned_rows, owned_rows,
-            pltpu.VMEM((n, shard, kv_width), jnp.bfloat16),
-            pltpu.VMEM((n, shard, kv_width), jnp.bfloat16),
+            pltpu.VMEM((n, 2, shard, HD), jnp.bfloat16),
+            pltpu.VMEM((2, shard, HD), jnp.bfloat16),
+            pltpu.VMEM((n, 2, 2, shard // n, HD), jnp.bfloat16),
+            pltpu.VMEM((n, 2, 2, shard // n, HD), jnp.bfloat16),
+            slab, slab, slab, slab, slab,
             pltpu.VMEM((4, q_width, width), jnp.bfloat16),
-            pltpu.VMEM((heads, shard, HD), jnp.float32),
-            pltpu.VMEM((heads, shard, 128), jnp.float32),
-            pltpu.VMEM((shard, q_width), jnp.bfloat16),
+            pltpu.VMEM((2 * heads, shard, HD), jnp.float32),
+            pltpu.VMEM((2 * heads, shard, 128), jnp.float32),
+            pltpu.VMEM((2, chunks, ROWS, group_cols), jnp.bfloat16),
+            pltpu.VMEM((chunks, ROWS, group_cols), jnp.bfloat16),
+            pltpu.VMEM((2, chunks, ROWS, group_cols), jnp.bfloat16),
+            pltpu.VMEM((2, chunks, ROWS, group_cols), jnp.bfloat16),
+            pltpu.VMEM((heads, 8, shard), jnp.float32),
+            pltpu.VMEM((heads, 8, shard), jnp.float32),
             half, half, half, half, half, half,
             pltpu.VMEM((chunks, ROWS, width), jnp.float32),
             pltpu.VMEM((8, shard), jnp.float32),
             pltpu.VMEM((4, 8, shard), jnp.float32),
-            pltpu.SemaphoreType.DMA((6,)),
-            pltpu.SemaphoreType.DMA((n, 2, 2)),
+            pltpu.SemaphoreType.DMA((9,)),
+            pltpu.SemaphoreType.DMA((4,)),
+            pltpu.SemaphoreType.DMA((3,)),
+            pltpu.SemaphoreType.DMA((3,)),
             pltpu.SemaphoreType.DMA((n, 2)),
-            pltpu.SemaphoreType.DMA((4,)),
+            pltpu.SemaphoreType.DMA((n, 2)),
+            pltpu.SemaphoreType.DMA((2,)),
+            pltpu.SemaphoreType.DMA((2,)),
+            pltpu.SemaphoreType.DMA((2, chunks)),
+            pltpu.SemaphoreType.DMA((2, chunks)),
+            pltpu.SemaphoreType.DMA((1,)),
+            pltpu.SemaphoreType.DMA((1,)),
+            pltpu.SemaphoreType.DMA((n,)),
+            pltpu.SemaphoreType.DMA((n,)),
+            pltpu.SemaphoreType.DMA((n // 2,)),
+            pltpu.SemaphoreType.DMA((n // 2,)),
+            pltpu.SemaphoreType.DMA((n // 2,)),
+            pltpu.SemaphoreType.DMA((n // 2,)),
+            pltpu.SemaphoreType.DMA((n // 2,)),
+            pltpu.SemaphoreType.DMA((chunks,)),
+            pltpu.SemaphoreType.DMA((chunks,)),
             pltpu.SemaphoreType.DMA((3, chunks)),
             pltpu.SemaphoreType.DMA((3, chunks)),
             pltpu.SemaphoreType.DMA((3,)),
             pltpu.SemaphoreType.DMA((4,)),
-            pltpu.SemaphoreType.DMA((n, 2)),
-            pltpu.SemaphoreType.DMA((n, 2)),
             pltpu.SemaphoreType.DMA((3,)),
         ],
         compiler_params=pltpu.CompilerParams(

time: 67.4 us -> 60.8 us (0.902)
  Pallas kernels: 66 us -> 59.4 us
    pallas_call x1, Pallas kernels: 63.8 us -> 57.2 us  [fused(): pl.pallas_call(functools.partial(layer_kernel, n), out_shape=(jax.ShapeDt...]
where the time goes in v1:
time: 60.8 us; the launch traced here: 60.6 us
  Pallas kernels  59.4 us (98%)
  between operations  1.29 us (2%)
    pallas_call x1, Pallas kernels, fused(): pl.pallas_call(functools.partial(layer_kernel, n), out_shape=(jax.ShapeDt...  57.2 us
    pallas_call x1, Pallas kernels, fused(): pl.pallas_call(put_out, out_shape=tuple((jax.ShapeDtypeStruct(a.shape, a....  2.2 us

profile of v1, /device:TPU:25, one launch (start us, length us, event | category | flops | bytes accessed | tf_op | source)
XLA Modules:
  0.0 60.6 jit_solution(11806953420039671232)
XLA Ops:
  1.3 57.2 %shard_map.103 = (bf16[256,896]{1,0:T(8,128)(2,1)}, bf16[512,512]{1,0:T(8,128)(2,1)}, bf16[512,512]{1,0:T(8,128)(2,1)}) custom-call(bf16[256,1024]{1,0:T(8,128)(2,1)} %bitcast.7, bf16[256,512]{1,0:T(8,128)(2,1)} %bitcast.9, bf16[256,512]{1,0:T(8,128)(2,1)} %bitcast.10, bf16[256,896]{1,0:T(8,128)(2,1)} %bitcast.8, f32[896]{0:T(1024)} %scale_hbm.1, ...), custom_call_target="tpu_custom_call" | custom-call | tf_op jit(solution)/shard_map/pallas_call | solution.py:751
  58.4 2.2 %shard_map.104 = (bf16[256,896]{1,0:T(8,128)(2,1)}, bf16[512,512]{1,0:T(8,128)(2,1)}, bf16[512,512]{1,0:T(8,128)(2,1)}) custom-call(bf16[256,896]{1,0:T(8,128)(2,1)} %get-tuple-element.9.refs_0_, bf16[512,512]{1,0:T(8,128)(2,1)} %get-tuple-element.10.refs_1_, bf16[512,512]{1,0:T(8,128)(2,1)} %get-tuple-element.11.refs_2_), custom_call_target="tpu_custom_call" | custom-call | tf_op jit(solution)/shard_map/pallas_call | solution.py:822

commit v2 on v1

v2 whole, which is shorter than its diff:
```python
import functools

import jax
import jax.numpy as jnp
from jax import lax
from jax.experimental import pallas as pl
from jax.experimental.pallas import tpu as pltpu
from jax.sharding import PartitionSpec as P

D = 3584
HD = 256
WINDOW = 4096
MESH = pl.DeviceIdType.MESH
LOG2E = 1.4426950408889634
ROWS = 64
LANES = 128


soft_cap = 50.0
norm_eps = 1e-06


def shifted(x, axis, by):
    peers = lax.axis_size(axis)
    pairs = [(i, i + by) for i in range(peers) if 0 <= i + by < peers]
    return lax.ppermute(x, axis, pairs)


def attend_block(grouped, block_keys, block_values, query_pos, key_pos, state_pair):
    numerator, denominator = state_pair
    seq_count, query_count, kv_local, group_size, head_size = grouped.shape
    keyed_rows = block_keys.reshape(seq_count, block_keys.shape[1], kv_local, head_size)
    valued_rows = block_values.reshape(seq_count, block_values.shape[1], kv_local, head_size)
    scores = jnp.einsum(
        "sqhgd,skhd->shgqk", grouped, keyed_rows, preferred_element_type=jnp.float32
    ) * head_size ** (-0.5)
    capped = soft_cap * jnp.tanh(scores / soft_cap)
    spread = query_pos[:, None] - key_pos[None, :]
    live_mask = (spread >= 0) & (spread < WINDOW) & (key_pos[None, :] >= 0)
    weights = jnp.where(live_mask, jnp.exp(capped), jnp.zeros_like(capped))
    denominator = denominator + jnp.sum(weights, axis=-1)
    numerator = numerator + jnp.einsum(
        "shgqk,skhd->sqhgd",
        weights.astype(jnp.bfloat16),
        valued_rows,
        preferred_element_type=jnp.float32,
    )
    return (numerator, denominator)


def reorder_blocks(blocked, ordering):
    return blocked[ordering]


def local(queries, key_rows, value_rows, residual, out_weight, post_scale, lengths, owners):
    seq_count, shard_len, query_width = queries.shape
    seq_size = lax.axis_size("seq")
    if (
        seq_count == 1 and lax.axis_size("tp") == 4 and seq_size % 2 == 0 and seq_size >= 6
        and seq_size * shard_len <= WINDOW and key_rows.shape[2] == 2 * HD
        and shard_len % LANES == 0
    ):
        return fused(
            seq_size, queries, key_rows, value_rows, residual, out_weight, post_scale, lengths,
            owners,
        )
    kv_width = key_rows.shape[2]
    kv_local = kv_width // HD
    group_size = query_width // kv_width
    grouped = queries.reshape(seq_count, shard_len, kv_local, group_size, HD)
    position = lax.axis_index("seq")
    seq_devices = lax.axis_size("seq")
    offsets = jnp.arange(shard_len, dtype=jnp.int32)
    query_pos = position * shard_len + offsets
    numerator = jnp.zeros((seq_count, shard_len, kv_local, group_size, HD), jnp.float32)
    denominator = jnp.zeros((seq_count, kv_local, group_size, shard_len), jnp.float32)
    state_pair = attend_block(
        grouped, key_rows, value_rows, query_pos, query_pos, (numerator, denominator)
    )
    hop_count = min(WINDOW // shard_len, seq_devices - 1)
    arrived = []
    current = (key_rows, value_rows)
    for hop_index in range(1, hop_count + 1):
        current = shifted((current[0], current[1]), "seq", 1)
        arrived.append((hop_index, current))
        if len(arrived) == 2 or hop_index == hop_count:
            ordered = arrived[::-1]
            block_keys = jnp.concatenate([member[1][0] for member in ordered], axis=1)
            block_values = jnp.concatenate([member[1][1] for member in ordered], axis=1)
            block_pos = jnp.concatenate(
                [(position - member[0]) * shard_len + offsets for member in ordered]
            )
            state_pair = attend_block(
                grouped, block_keys, block_values, query_pos, block_pos, state_pair
            )
            arrived = []
    numerator, denominator = state_pair
    attended = (numerator / jnp.transpose(denominator, (0, 3, 1, 2))[..., None]).astype(
        jnp.bfloat16
    )
    partial_value = jnp.dot(
        attended.reshape(seq_count * shard_len, query_width),
        out_weight,
        preferred_element_type=jnp.float32,
    )
    partial_value = partial_value.reshape(seq_count, shard_len, out_weight.shape[1])
    branch = lax.psum_scatter(partial_value, "tp", scatter_dimension=2, tiled=True)
    squares = lax.psum(jnp.sum(branch * branch, axis=-1), "tp")
    normed = branch * lax.rsqrt(squares / D + norm_eps)[..., None] * post_scale
    hidden_out = (residual.astype(jnp.float32) + normed).astype(jnp.bfloat16)
    block_rows = shard_len // seq_devices
    slot_span = WINDOW // shard_len
    live_rows = (query_pos[None, :] >= lengths[:, None] - WINDOW) & (
        query_pos[None, :] < lengths[:, None]
    )
    kept_keys = jnp.where(live_rows[..., None], key_rows, jnp.zeros_like(key_rows))
    kept_values = jnp.where(live_rows[..., None], value_rows, jnp.zeros_like(value_rows))
    devices = jnp.arange(seq_devices, dtype=jnp.int32)
    matches = owners[:, :, None] == devices[None, None, :]
    inverse = jnp.sum(
        jnp.where(matches, devices[None, :, None], jnp.zeros_like(devices)[None, :, None]), axis=1
    )
    outgoing_keys = jax.vmap(reorder_blocks)(
        kept_keys.reshape(seq_count, seq_devices, block_rows, kv_width), inverse
    )
    outgoing_values = jax.vmap(reorder_blocks)(
        kept_values.reshape(seq_count, seq_devices, block_rows, kv_width), inverse
    )
    incoming = (
        lax.all_to_all(outgoing_keys, "seq", split_axis=1, concat_axis=1, tiled=True),
        lax.all_to_all(outgoing_values, "seq", split_axis=1, concat_axis=1, tiled=True),
    )
    selector = (
        devices[None, :] % slot_span == jnp.arange(slot_span, dtype=jnp.int32)[:, None]
    ).astype(jnp.bfloat16)
    cache_keys = (
        jnp.einsum("md,sdbf->smbf", selector, incoming[0], preferred_element_type=jnp.float32)
        .astype(jnp.bfloat16)
        .reshape(seq_count, slot_span * block_rows, kv_width)
    )
    cache_values = (
        jnp.einsum("md,sdbf->smbf", selector, incoming[1], preferred_element_type=jnp.float32)
        .astype(jnp.bfloat16)
        .reshape(seq_count, slot_span * block_rows, kv_width)
    )
    return (hidden_out, cache_keys, cache_values)


def layer_kernel(
    n, q_hbm, k_hbm, v_hbm, res_hbm, scale_hbm, len_ref, own_hbm, w_ref,
    hid_ref, ck_ref, cv_ref,
    qall, qpart, res_ref, scale_ref, own_ref, kv, other,
    down_out, down_in, pair_out, pair_in, line_out, line_in, skew_out,
    wbuf, acc, den, att, att_out, lent_out,
    to_sib, to_x, to_sib2, from_sib, from_x, from_sib2, early, total, folds, sq_out, sq_in,
    in_sem, w_sem, y_send, yq_send, y_recv, z_send, z_recv, lend_recv, q_send, q_recv, lent_send,
    down_send, down_recv, pair_send, pair_recv, line_send, line_recv, skew_send, att_send, att_recv,
    rs_send, rs_recv, sib2_recv, sq_send, sq_recv,
):
    nz = n // 2
    top = nz - 1
    me = lax.axis_index("seq")
    t = lax.axis_index("tp")
    z, y = me // 2, me % 2
    x, c = t // 2, t % 2
    sib = x * 2 + (1 - c)
    across = (1 - x) * 2 + c
    diagonal = (1 - x) * 2 + (1 - c)
    partner = z * 2 + (1 - y)
    shard = kv.shape[2]
    width = res_ref.shape[1]
    group_cols = qpart.shape[1]
    group = group_cols // HD
    block_rows = shard // n
    chunks = shard // ROWS
    lends = (c == 1) & (z == top)
    hosts = (c == 1) & (z == top - 1)
    takes_kv = (z < top) | (c == 0)
    sends_kv = (z < top - 1) | ((z < top) & (c == 0))

    def half(ref, which, cols):
        return ref.at[:, pl.ds(pl.multiple_of(which * cols, cols), cols)]

    loads = [
        pltpu.make_async_copy(src, dst, in_sem.at[i])
        for i, (src, dst) in enumerate(
            (
                (half(k_hbm, 1 - y, HD), other.at[0]), (half(v_hbm, 1 - y, HD), other.at[1]),
                (half(k_hbm, y, HD), kv.at[me, 0]), (half(v_hbm, y, HD), kv.at[me, 1]),
                (half(q_hbm, 1 - y, group_cols), qpart), (half(q_hbm, y, group_cols), qall.at[y]),
                (own_hbm, own_ref), (res_hbm, res_ref), (scale_hbm, scale_ref),
            )
        )
    ]
    for load in loads[:7]:
        load.start()

    barrier = pltpu.get_barrier_semaphore()
    for peer in (sib, across, diagonal):
        pl.semaphore_signal(barrier, inc=1, device_id={"tp": peer}, device_id_type=MESH)
    for hop in range(1, n):
        pl.semaphore_signal(
            barrier, inc=1, device_id={"seq": lax.rem(me + hop, n)}, device_id_type=MESH
        )

    def clear(s, carry):
        acc[s] = jnp.zeros(acc.shape[1:], jnp.float32)
        den[s] = jnp.zeros(den.shape[1:], jnp.float32)
        return carry

    lax.fori_loop(0, acc.shape[0], clear, 0)
    pl.semaphore_wait(barrier, n + 2)

    def remote(src, dst, send, recv, to):
        return pltpu.make_async_remote_copy(
            src_ref=src, dst_ref=dst, send_sem=send, recv_sem=recv, device_id=to,
            device_id_type=MESH,
        )

    def settle(ref, sem):
        pltpu.make_async_copy(ref, ref, sem.at[0]).wait()

    def y_copy(h, origin):
        return remote(
            other.at[h], kv.at[origin, h], y_send.at[0], y_recv.at[h], {"seq": partner}
        )

    def yq_copy(slot):
        return remote(qpart, qall.at[slot], yq_send.at[0], y_recv.at[2], {"seq": partner})

    def z_copy(origin, h):
        return remote(
            kv.at[origin, h], kv.at[origin, h], z_send.at[0], z_recv.at[origin, h],
            {"seq": me + 2},
        )

    def lend_copy(yq):
        return remote(
            qall.at[yq], qall.at[2 + yq], q_send.at[0], q_recv.at[0], {"seq": me - 2}
        )

    def lend_kv(origin, h):
        return remote(
            kv.at[origin, h], kv.at[origin, h], z_send.at[0], lend_recv.at[0],
            {"seq": me - 2},
        )

    def w_copy(f, g):
        return pltpu.make_async_copy(
            w_ref.at[pl.ds(g * group_cols, group_cols), pl.ds(f * width, width)],
            wbuf.at[f, g], w_sem.at[0],
        )

    for h in (0, 1):
        loads[2 + h].wait()
        pl.when(sends_kv)(z_copy(me, h).start)
    for load in (loads[0], loads[1], loads[4], loads[5]):
        load.wait()

    @pl.when(z == top)
    def _():
        yq_copy(y).start()
        for h in (0, 1):
            y_copy(h, me).start()

    @pl.when(z < top)
    def _():
        for h in (0, 1):
            y_copy(h, me).start()
        yq_copy(y).start()

    @pl.when(lends)
    def _():
        lend_copy(y).start()
        for h in (0, 1):
            lend_kv(me, h).start()

    loads[6].wait()
    for f in range(4):
        for g in (0, 1):
            w_copy(f, g).start()
    for load in loads[7:]:
        load.start()

    def owned(device):
        block = own_ref[0, 0] * 0
        for b in range(n):
            block = block + jnp.where(own_ref[0, b] == device, b, 0)
        return jnp.full((block_rows, HD), block, jnp.int32)

    def select(ref, lead, chosen):
        got = jnp.zeros(chosen.shape, jnp.float32)
        for b in range(n):
            rows = ref[(*lead, slice(b * block_rows, (b + 1) * block_rows))]
            got = jnp.where(chosen == b, rows.astype(jnp.float32), got)
        return got.astype(jnp.bfloat16)

    def down_copy(to, slot):
        return remote(
            down_out.at[to], down_in.at[slot], down_send.at[0], down_recv.at[0], {"seq": to}
        )

    def stage(to, carry):
        chosen = owned(to)
        for h in (0, 1):
            down_out[to, h, y] = select(kv, (me, h), chosen)
            down_out[to, h, 1 - y] = select(other, (h,), chosen)
        return carry

    def post(to, carry):
        down_copy(to, me).start()
        return carry

    lax.fori_loop(0, 2 * z, stage, 0)

    @pl.when(lends)
    def _():
        yq_copy(1 - y).wait_recv()
        lend_copy(1 - y).start()

    for h in (0, 1):
        y_copy(h, partner).wait_recv()
        pl.when(sends_kv)(z_copy(partner, h).start)
        pl.when(lends)(lend_kv(partner, h).start)
    lax.fori_loop(0, 2 * z, post, 0)

    def take(d, j):
        origin = 2 * (z - d) + jnp.where(j == 0, y, 1 - y)
        for h in (0, 1):
            z_copy(origin, h).wait_recv()
            pl.when(sends_kv)(z_copy(origin, h).start)

    @pl.when((z > 0) & takes_kv)
    def _():
        take(1, 0)
        take(1, 1)

    @pl.when(jnp.logical_not(lends))
    def _():
        yq_copy(1 - y).wait_recv()

    def attend(base, origin, above):
        pair = pl.ds(base, 2)
        for hh in range(group):
            stacked = qall[pair, :, hh * HD : (hh + 1) * HD].reshape(2 * shard, HD)
            scores = lax.dot_general(
                stacked, kv[origin, 0], (((1,), (1,)), ((), ())),
                preferred_element_type=jnp.float32,
            )
            w = jnp.exp2(jnp.tanh(scores * (HD ** (-0.5) / soft_cap)) * (soft_cap * LOG2E))
            if above is not None:
                keep = lax.broadcasted_iota(jnp.int32, w.shape, 0) >= above + (
                    lax.broadcasted_iota(jnp.int32, w.shape, 1)
                )
                w = jnp.where(keep, w, 0.0)
            folded = w[:, :LANES]
            for i in range(1, w.shape[1] // LANES):
                folded = folded + w[:, i * LANES : (i + 1) * LANES]
            den[hh, pair] += folded.reshape(2, shard, LANES)
            acc[hh, pair] += jnp.dot(
                w.astype(jnp.bfloat16), kv[origin, 1], preferred_element_type=jnp.float32
            ).reshape(2, shard, HD)

    def own_slab(base, slab):
        def diagonal_block(i, carry):
            attend(base, 2 * slab + i, i * shard)
            return carry

        lax.fori_loop(0, 2, diagonal_block, 0)

    pl.when(jnp.logical_not(lends))(functools.partial(own_slab, 0, z))
    @pl.when(hosts)
    def _():
        settle(qall.at[2:], q_recv)

        def one(i, carry):
            attend(2, 2 * z + i, None)
            return carry

        lax.fori_loop(0, 2, one, 0)

    def pair_copy(zo):
        return remote(
            pair_out.at[zo], pair_in.at[zo], pair_send.at[0], pair_recv.at[0], {"seq": partner}
        )

    def line_copy(zo):
        return remote(
            line_out.at[zo], line_in.at[zo], line_send.at[0], line_recv.at[0], {"seq": me + 2}
        )

    def skew_copy(zo):
        return remote(
            skew_out.at[zo], pair_in.at[zo], skew_send.at[0], pair_recv.at[0],
            {"seq": partner + 2},
        )

    def gather(zo, device, out):
        chosen = owned(device)
        for yo in (0, 1):
            for h in (0, 1):
                out[zo, yo, h] = select(kv, (2 * zo + yo, h), chosen)

    def pass_cache(zo):
        @pl.when((zo == z) | takes_kv)
        def _():
            gather(zo, partner, pair_out)
            pair_copy(zo).start()

        @pl.when(hosts)
        def _():
            gather(zo, me + 2, line_out)
            line_copy(zo).start()
            gather(zo, partner + 2, skew_out)
            skew_copy(zo).start()

    pairs = jnp.where(hosts, 2, 1)

    def phase(d, carry):
        @pl.when(z - d + 1 >= 1)
        def _():
            pass_cache(z - d + 1)

        @pl.when(hosts & (d == jnp.minimum(2, z)))
        def _():
            settle(kv.at[2 * top :], lend_recv)
            own_slab(2, top)

        def side(j, carry):
            @pl.when((z - d >= 0) & takes_kv)
            def _():
                @pl.when(d > 1)
                def _():
                    take(d, j)

                origin = 2 * (z - d) + jnp.where(j == 0, y, 1 - y)

                def one(i, carry):
                    attend(2 * i, origin, None)
                    return carry

                lax.fori_loop(0, pairs, one, 0)

            return carry

        lax.fori_loop(0, 2, side, 0)
        return carry

    lax.fori_loop(1, nz, phase, 0)

    def rows_of(r):
        return pl.ds(pl.multiple_of(r * ROWS, ROWS), ROWS)

    def att_copy(r, g):
        return remote(
            att_out.at[r], att.at[g, r], att_send.at[0], att_recv.at[r], {"seq": partner}
        )

    def lent_copy(yq, r, g):
        return remote(
            lent_out.at[yq, r], att.at[g, r], lent_send.at[0], att_recv.at[r],
            {"seq": 2 * top + yq},
        )

    def finish(s, r, out, lead):
        for hh in range(group):
            out[(*lead, slice(None), slice(hh * HD, (hh + 1) * HD))] = (
                acc[hh, s, rows_of(r), :]
                / jnp.sum(den[hh, s, rows_of(r), :], axis=-1, keepdims=True)
            ).astype(jnp.bfloat16)

    def away(r, carry):
        finish(1 - y, r, att_out, (r,))
        att_copy(r, y).start()
        return carry

    def home(r, carry):
        finish(y, r, att, (y, r))
        return carry

    def give(r, carry):
        for yq in (1 - y, y):
            finish(2 + yq, r, lent_out, (yq, r))
            lent_copy(yq, r, y).start()
        return carry

    @pl.when(jnp.logical_not(lends))
    def _():
        lax.fori_loop(0, chunks, away, 0)
        lax.fori_loop(0, chunks, home, 0)

    def rs_copy(kind, r, src, dst, recv, to):
        return remote(src.at[r], dst.at[r], rs_send.at[kind], recv, {"tp": to})

    def sib_copy(r):
        return rs_copy(0, r, to_sib, from_sib, rs_recv.at[0, r], sib)

    def x_copy(r):
        return rs_copy(1, r, to_x, from_x, rs_recv.at[1, r], across)

    def sib2_copy(r):
        return rs_copy(2, r, to_sib2, from_sib2, sib2_recv.at[0], sib)

    def product(rows, f, g):
        return jnp.dot(rows, wbuf[f, g], preferred_element_type=jnp.float32)

    def part(f, r):
        pair = pl.ds(2 * r, 2)
        rows = [att[g, pair].reshape(2 * ROWS, group_cols) for g in (0, 1)]
        return product(rows[0], f, 0) + product(rows[1], f, 1)

    settle(wbuf, w_sem)

    sent = (diagonal, across)

    @pl.when(jnp.logical_not(lends))
    def _():
        for i, f in enumerate(sent):
            early[i] = product(att[y].reshape(shard, group_cols), f, y)

    @pl.when(hosts)
    def _():
        lax.fori_loop(0, chunks, give, 0)

    def send_sib(r):
        pl.when(jnp.logical_not(lends))(att_copy(r, 1 - y).wait_recv)

        @pl.when(lends)
        def _():
            both_heads = att.at[:, r]
            pltpu.make_async_copy(both_heads, both_heads, att_recv.at[r]).wait()
            for i, f in enumerate(sent):
                early[i, rows_of(r), :] = product(att[y, r], f, y)

        to_sib[r] = (early[0, rows_of(r), :] + product(att[1 - y, r], diagonal, 1 - y)).astype(
            jnp.bfloat16
        )
        sib_copy(r).start()

    def send_x(r):
        mine = early[1, rows_of(r), :] + product(att[1 - y, r], across, 1 - y)
        sib_copy(r).wait_recv()
        to_x[r] = (mine + from_sib[r].astype(jnp.float32)).astype(jnp.bfloat16)
        x_copy(r).start()

    def both(r, carry):
        pl.when(r < chunks)(functools.partial(send_sib, r))
        pl.when(r > 0)(functools.partial(send_x, r - 1))
        return carry

    def third(r, carry):
        pair = pl.ds(2 * r, 2)
        to_sib2[pair] = part(sib, r).astype(jnp.bfloat16).reshape(2, ROWS, width)
        for i in (0, 1):
            sib2_copy(2 * r + i).start()
        return carry

    def fourth(r, carry):
        rows = pl.ds(pl.multiple_of(2 * r * ROWS, 2 * ROWS), 2 * ROWS)
        total[rows, :] = part(t, r)
        return carry

    lax.fori_loop(0, chunks + 1, both, 0)

    pass_cache(0)

    for step in (third, fourth):
        lax.fori_loop(0, chunks // 2, step, 0)

    mine_blocks = owned(me)
    local_row = lax.broadcasted_iota(jnp.int32, mine_blocks.shape, 0)
    bound = jnp.full(mine_blocks.shape, len_ref[0], jnp.int32)

    for slab in range(nz):

        @pl.when(z == slab)
        def _():
            settle(pair_in.at[: slab + 1], pair_recv)
            if slab < top:
                settle(down_in.at[2 * slab + 2 :], down_recv)

    @pl.when(lends)
    def _():
        settle(line_in.at[:top], line_recv)

    def cache(zo, carry):
        far = lends & (zo < top)

        for yo in (0, 1):
            origin = 2 * zo + yo
            pos = local_row + mine_blocks * block_rows + origin * shard
            live = (pos < bound) & (pos >= bound - WINDOW)
            rows = pl.ds(pl.multiple_of(origin * block_rows, block_rows), block_rows)

            for h, out in enumerate((ck_ref, cv_ref)):

                def put(g, value):
                    cols = pl.ds(pl.multiple_of(g * HD, HD), HD)
                    out[rows, cols] = jnp.where(live, value.astype(jnp.float32), 0.0).astype(
                        jnp.bfloat16
                    )

                @pl.when(zo > z)
                def _():
                    for g in (0, 1):
                        put(g, down_in[origin, h, g])

                @pl.when(zo <= z)
                def _():
                    put(1 - y, pair_in[zo, yo, h])

                @pl.when((zo <= z) & jnp.logical_not(far))
                def _():
                    put(y, select(kv, (origin, h), mine_blocks))

                @pl.when(far)
                def _():
                    put(y, line_in[zo, yo, h])

        return carry

    lax.fori_loop(0, nz, cache, 0)
    rest = ck_ref.shape[0] - n * block_rows
    if rest:
        for out in (ck_ref, cv_ref):
            out[n * block_rows :, :] = jnp.zeros((rest, 2 * HD), jnp.bfloat16)
    settle(from_sib2, sib2_recv)
    for r in range(chunks):
        x_copy(r).wait_recv()
        rows = slice(r * ROWS, (r + 1) * ROWS)
        branch = total[rows, :] + from_sib2[r].astype(jnp.float32) + from_x[r].astype(jnp.float32)
        total[rows, :] = branch
        squared = branch * branch
        folded = squared[:, :LANES]
        for i in range(1, width // LANES):
            folded = folded + squared[:, i * LANES : (i + 1) * LANES]
        folds[rows, :] = folded
        if (r + 1) * ROWS % LANES == 0:
            rows = slice((r + 1) * ROWS - LANES, (r + 1) * ROWS)
            line = jnp.sum(folds[rows, :].T, axis=0, keepdims=True)
            sq_out[:, rows] = jnp.broadcast_to(line, (8, LANES))

    def sq_copy(i, to, slot):
        return pltpu.make_async_remote_copy(
            src_ref=sq_out, dst_ref=sq_in.at[slot], send_sem=sq_send.at[0],
            recv_sem=sq_recv.at[0], device_id={"tp": to}, device_id_type=MESH,
        )

    peers = (sib, across, diagonal)
    for i, peer in enumerate(peers):
        sq_copy(i, peer, t).start()
    squares = sq_out[...]
    settle(sq_in.at[:3], sq_recv)
    for i, peer in enumerate(peers):
        squares = squares + sq_in[peer]
    loads[7].wait()
    loads[8].wait()
    factor = lax.rsqrt(squares / D + norm_eps)
    for r in range(shard // LANES):
        rows = slice(r * LANES, (r + 1) * LANES)
        spread = jnp.broadcast_to(factor[:1, rows], (LANES, LANES)).T
        for i in range(width // LANES):
            cols = slice(i * LANES, (i + 1) * LANES)
            normed = total[rows, cols] * spread * scale_ref[cols].reshape(1, LANES)
            hid_ref[rows, cols] = (res_ref[rows, cols].astype(jnp.float32) + normed).astype(
                jnp.bfloat16
            )

    settle(sq_in.at[:3], sq_send)
    for kind, sent_rows in enumerate((to_sib, to_x, to_sib2)):
        pltpu.make_async_copy(sent_rows, sent_rows, rs_send.at[kind]).wait()
    settle(other, y_send)
    settle(qpart, yq_send)
    for slab in range(nz):

        @pl.when((z == slab) & sends_kv)
        def _():
            settle(kv.at[: 2 * slab + 2], z_send)

        @pl.when((z == slab) & takes_kv)
        def _():
            settle(pair_out.at[: slab + 1], pair_send)

        if slab:

            @pl.when(z == slab)
            def _():
                settle(down_out.at[: 2 * slab], down_send)

    @pl.when(lends)
    def _():
        settle(qall.at[:2], q_send)
        settle(kv.at[2 * top :], z_send)
        settle(pair_out.at[top:], pair_send)

    @pl.when(jnp.logical_not(lends))
    def _():
        settle(att_out, att_send)

    @pl.when(hosts)
    def _():
        settle(lent_out, lent_send)
        settle(line_out.at[:top], line_send)
        settle(skew_out.at[:top], skew_send)


def put_out(*refs):
    count = (len(refs) - 1) // 2
    copies = [
        pltpu.make_async_copy(refs[i], refs[count + i], refs[-1].at[i]) for i in range(count)
    ]
    for copy in copies:
        copy.start()
    for copy in copies:
        copy.wait()


def fused(n, queries, key_rows, value_rows, residual, out_weight, post_scale, lengths, owners):
    shard, q_width = queries.shape[1:]
    kv_width = key_rows.shape[2]
    width = residual.shape[2]
    chunks = shard // ROWS
    cache_rows = WINDOW // n
    smem = pl.BlockSpec(memory_space=pltpu.SMEM)
    apart = pl.BlockSpec(memory_space=pl.ANY)
    held = pl.BlockSpec(memory_space=pltpu.VMEM)
    one = pltpu.SemaphoreType.DMA((1,))
    group_cols = q_width * HD // kv_width
    slab = pltpu.VMEM((n // 2, 2, 2, shard // n, HD), jnp.bfloat16)
    half = pltpu.VMEM((chunks, ROWS, width), jnp.bfloat16)
    hidden, ck, cv = pl.pallas_call(
        functools.partial(layer_kernel, n),
        out_shape=(
            pltpu.VMEM((shard, width), jnp.bfloat16),
            pltpu.VMEM((cache_rows, kv_width), jnp.bfloat16),
            pltpu.VMEM((cache_rows, kv_width), jnp.bfloat16),
        ),
        in_specs=[apart] * 5 + [smem] + [apart] * 2,
        out_specs=(held,) * 3,
        scratch_shapes=[
            pltpu.VMEM((4, shard, group_cols), jnp.bfloat16),
            pltpu.VMEM((shard, group_cols), jnp.bfloat16),
            pltpu.VMEM((shard, width), jnp.bfloat16),
            pltpu.VMEM((width,), jnp.float32),
            pltpu.SMEM((1, n), jnp.int32),
            pltpu.VMEM((n, 2, shard, HD), jnp.bfloat16),
            pltpu.VMEM((2, shard, HD), jnp.bfloat16),
            pltpu.VMEM((n, 2, 2, shard // n, HD), jnp.bfloat16),
            pltpu.VMEM((n, 2, 2, shard // n, HD), jnp.bfloat16),
            slab, slab, slab, slab, slab,
            pltpu.VMEM((4, 2, group_cols, width), jnp.bfloat16),
            pltpu.VMEM((group_cols // HD, 4, shard, HD), jnp.float32),
            pltpu.VMEM((group_cols // HD, 4, shard, LANES), jnp.float32),
            pltpu.VMEM((2, chunks, ROWS, group_cols), jnp.bfloat16),
            pltpu.VMEM((chunks, ROWS, group_cols), jnp.bfloat16),
            pltpu.VMEM((2, chunks, ROWS, group_cols), jnp.bfloat16),
            half, half, half, half, half, half,
            pltpu.VMEM((2, shard, width), jnp.float32),
            pltpu.VMEM((shard, width), jnp.float32),
            pltpu.VMEM((shard, LANES), jnp.float32),
            pltpu.VMEM((8, shard), jnp.float32),
            pltpu.VMEM((4, 8, shard), jnp.float32),
            pltpu.SemaphoreType.DMA((9,)),
            one,
            one,
            one,
            pltpu.SemaphoreType.DMA((3,)),
            one,
            pltpu.SemaphoreType.DMA((n - 2, 2)),
            one,
            one,
            one,
            one,
            one,
            one,
            one,
            one,
            one,
            one,
            one,
            one,
            pltpu.SemaphoreType.DMA((chunks,)),
            pltpu.SemaphoreType.DMA((3,)),
            pltpu.SemaphoreType.DMA((2, chunks)),
            one,
            one,
            one,
        ],
        compiler_params=pltpu.CompilerParams(
            collective_id=0, has_side_effects=True, vmem_limit_bytes=62 * 1024 * 1024
        ),
    )(
        queries[0], key_rows[0], value_rows[0], residual[0], post_scale, lengths, owners,
        out_weight,
    )
    made = (hidden, ck, cv)
    hidden, ck, cv = pl.pallas_call(
        put_out,
        out_shape=tuple(jax.ShapeDtypeStruct(a.shape, a.dtype) for a in made),
        in_specs=[apart] * len(made),
        out_specs=(apart,) * len(made),
        scratch_shapes=[pltpu.SemaphoreType.DMA((len(made),))],
    )(*(pltpu.with_memory_space_constraint(a, pltpu.VMEM) for a in made))
    return hidden[None], ck[None], cv[None]


def solution(mesh):
    placed = (
        P(None, "seq", "tp"),
        P(None, "seq", "tp"),
        P(None, "seq", "tp"),
        P(None, "seq", "tp"),
        P("tp", None),
        P("tp"),
        P(),
        P(),
    )
    return jax.shard_map(
        local,
        mesh=mesh,
        in_specs=placed,
        out_specs=(P(None, "seq", "tp"), P(None, "seq", "tp"), P(None, "seq", "tp")),
        check_vma=False,
    )
```

time: 60.8 us -> 54.3 us (0.89)
  Pallas kernels: 59.4 us -> 52.8 us
    pallas_call x1, Pallas kernels: 57.2 us -> 51.7 us  [fused(): pl.pallas_call(functools.partial(layer_kernel, n), out_shape=(pltpu.VMEM(...]
    pallas_call x1, Pallas kernels: 2.2 us -> 1.15 us  [fused(): pl.pallas_call(put_out, out_shape=tuple((jax.ShapeDtypeStruct(a.shape, a....]
where the time goes in v2:
time: 54.3 us; the launch traced here: 54.1 us
  Pallas kernels  52.8 us (97%)
  between operations  1.29 us (2%)
    pallas_call x1, Pallas kernels, fused(): pl.pallas_call(functools.partial(layer_kernel, n), out_shape=(pltpu.VMEM(...  51.7 us
    pallas_call x1, Pallas kernels, fused(): pl.pallas_call(put_out, out_shape=tuple((jax.ShapeDtypeStruct(a.shape, a....  1.15 us

profile of v2, /device:TPU:25, one launch (start us, length us, event | category | flops | bytes accessed | tf_op | source)
XLA Modules:
  0.0 54.1 jit_solution(16530744414957127961)
XLA Ops:
  1.3 51.7 %shard_map.103 = (bf16[256,896]{1,0:T(8,128)(2,1)S(1)}, bf16[512,512]{1,0:T(8,128)(2,1)S(1)}, bf16[512,512]{1,0:T(8,128)(2,1)S(1)}) custom-call(bf16[256,1024]{1,0:T(8,128)(2,1)} %bitcast.7, bf16[256,512]{1,0:T(8,128)(2,1)} %bitcast.9, bf16[256,512]{1,0:T(8,128)(2,1)} %bitcast.10, bf16[256,896]{1,0:T(8,128)(2,1)} %bitcast.8, f32[896]{0:T(1024)} %scale_hbm.1, ...), custom_call_target="tpu_custom_call" | custom-call | tf_op jit(solution)/shard_map/pallas_call | solution.py:731
  53.0 1.1 %shard_map.104 = (bf16[256,896]{1,0:T(8,128)(2,1)}, bf16[512,512]{1,0:T(8,128)(2,1)}, bf16[512,512]{1,0:T(8,128)(2,1)}) custom-call(bf16[256,896]{1,0:T(8,128)(2,1)S(1)} %get-tuple-element.9.refs_0_, bf16[512,512]{1,0:T(8,128)(2,1)S(1)} %get-tuple-element.10.refs_1_, bf16[512,512]{1,0:T(8,128)(2,1)S(1)} %get-tuple-element.11.refs_2_), custom_call_target="tpu_custom_call" | custom-call | tf_op jit(solution)/shard_map/pallas_call | solution.py:797

commit v3 on v2

--- a/solution.py
+++ b/solution.py
@@ -12,7 +12,7 @@
 WINDOW = 4096
 MESH = pl.DeviceIdType.MESH
 LOG2E = 1.4426950408889634
-ROWS = 64
+ROWS = 32
 LANES = 128
 
 
@@ -56,7 +56,7 @@
     seq_count, shard_len, query_width = queries.shape
     seq_size = lax.axis_size("seq")
     if (
-        seq_count == 1 and lax.axis_size("tp") == 4 and seq_size % 2 == 0 and seq_size >= 6
+        seq_count == 1 and lax.axis_size("tp") == 4 and seq_size % 2 == 0 and seq_size >= 8
         and seq_size * shard_len <= WINDOW and key_rows.shape[2] == 2 * HD
         and shard_len % LANES == 0
     ):
@@ -151,11 +151,11 @@
     hid_ref, ck_ref, cv_ref,
     qall, qpart, res_ref, scale_ref, own_ref, kv, other,
     down_out, down_in, pair_out, pair_in, line_out, line_in, skew_out,
-    wbuf, acc, den, att, att_out, lent_out,
+    wbuf, acc, den, rounded, att, att_out, lent_out,
     to_sib, to_x, to_sib2, from_sib, from_x, from_sib2, early, total, folds, sq_out, sq_in,
     in_sem, w_sem, y_send, yq_send, y_recv, z_send, z_recv, lend_recv, q_send, q_recv, lent_send,
     down_send, down_recv, pair_send, pair_recv, line_send, line_recv, skew_send, att_send, att_recv,
-    rs_send, rs_recv, sib2_recv, sq_send, sq_recv,
+    rs_send, rs_recv, sib2_recv, sq_send, sq_recv, turn,
 ):
     nz = n // 2
     top = nz - 1
@@ -173,10 +173,14 @@
     group = group_cols // HD
     block_rows = shard // n
     chunks = shard // ROWS
+    merge = LANES // ROWS
     lends = (c == 1) & (z == top)
     hosts = (c == 1) & (z == top - 1)
     takes_kv = (z < top) | (c == 0)
     sends_kv = (z < top - 1) | ((z < top) & (c == 0))
+
+    frees = (c == 0) & (z == top - 2)
+    defers = (c == 1) & (z == top - 2)
 
     def half(ref, which, cols):
         return ref.at[:, pl.ds(pl.multiple_of(which * cols, cols), cols)]
@@ -313,6 +317,40 @@
 
     lax.fori_loop(0, 2 * z, stage, 0)
 
+    def pair_copy(zo):
+        return remote(
+            pair_out.at[zo], pair_in.at[zo], pair_send.at[0], pair_recv.at[0], {"seq": partner}
+        )
+
+    def line_copy(zo):
+        return remote(
+            line_out.at[zo], line_in.at[zo], line_send.at[0], line_recv.at[0], {"seq": me + 2}
+        )
+
+    def skew_copy(zo):
+        return remote(
+            skew_out.at[zo], pair_in.at[zo], skew_send.at[0], pair_recv.at[0],
+            {"seq": partner + 2},
+        )
+
+    def gather(zo, device, out):
+        chosen = owned(device)
+        for yo in (0, 1):
+            for h in (0, 1):
+                out[zo, yo, h] = select(kv, (2 * zo + yo, h), chosen)
+
+    def pass_cache(zo):
+        @pl.when((zo == z) | takes_kv)
+        def _():
+            gather(zo, partner, pair_out)
+            pair_copy(zo).start()
+
+    def lift_cache(zo):
+        gather(zo, me + 2, line_out)
+        line_copy(zo).start()
+        gather(zo, partner + 2, skew_out)
+        skew_copy(zo).start()
+
     @pl.when(lends)
     def _():
         yq_copy(1 - y).wait_recv()
@@ -324,16 +362,22 @@
         pl.when(lends)(lend_kv(partner, h).start)
     lax.fori_loop(0, 2 * z, post, 0)
 
-    def take(d, j):
-        origin = 2 * (z - d) + jnp.where(j == 0, y, 1 - y)
-        for h in (0, 1):
-            z_copy(origin, h).wait_recv()
-            pl.when(sends_kv)(z_copy(origin, h).start)
+    pl.when(hosts)(functools.partial(lift_cache, z))
+
+    def take(origin, h):
+        z_copy(origin, h).wait_recv()
+        held_back = defers & (origin == 1 - y)
+        pl.when(sends_kv & jnp.logical_not(held_back))(z_copy(origin, h).start)
 
     @pl.when((z > 0) & takes_kv)
     def _():
-        take(1, 0)
-        take(1, 1)
+        for origin in (me - 2, partner - 2):
+            for h in (0, 1):
+                take(origin, h)
+
+    @pl.when(hosts & (z > 1))
+    def _():
+        lift_cache(z - 1)
 
     @pl.when(jnp.logical_not(lends))
     def _():
@@ -361,6 +405,39 @@
                 w.astype(jnp.bfloat16), kv[origin, 1], preferred_element_type=jnp.float32
             ).reshape(2, shard, HD)
 
+    def weigh(i, origin):
+        pair = pl.ds(2 * i, 2)
+        for hh in range(group):
+            stacked = qall[pair, :, hh * HD : (hh + 1) * HD].reshape(2 * shard, HD)
+            scores = lax.dot_general(
+                stacked, kv[origin, 0], (((1,), (1,)), ((), ())),
+                preferred_element_type=jnp.float32,
+            )
+            w = jnp.exp2(jnp.tanh(scores * (HD ** (-0.5) / soft_cap)) * (soft_cap * LOG2E))
+            folded = w[:, :LANES]
+            for j in range(1, w.shape[1] // LANES):
+                folded = folded + w[:, j * LANES : (j + 1) * LANES]
+            den[hh, pair] += folded.reshape(2, shard, LANES)
+            rounded[i, hh] = w.astype(jnp.bfloat16)
+
+    def mix(i, origin):
+        pair = pl.ds(2 * i, 2)
+        for hh in range(group):
+            acc[hh, pair] += jnp.dot(
+                rounded[i, hh], kv[origin, 1], preferred_element_type=jnp.float32
+            ).reshape(2, shard, HD)
+
+    def invert():
+        def one(i, carry):
+            pair = pl.ds(2 * i, 2)
+            for hh in range(group):
+                whole = den[hh, pair].reshape(2 * shard, LANES)
+                inverse = 1.0 / jnp.sum(whole, axis=-1, keepdims=True)
+                den[hh, pair] = jnp.broadcast_to(inverse, whole.shape).reshape(2, shard, LANES)
+            return carry
+
+        lax.fori_loop(0, jnp.where(hosts, 2, 1), one, 0)
+
     def own_slab(base, slab):
         def diagonal_block(i, carry):
             attend(base, 2 * slab + i, i * shard)
@@ -379,41 +456,6 @@
 
         lax.fori_loop(0, 2, one, 0)
 
-    def pair_copy(zo):
-        return remote(
-            pair_out.at[zo], pair_in.at[zo], pair_send.at[0], pair_recv.at[0], {"seq": partner}
-        )
-
-    def line_copy(zo):
-        return remote(
-            line_out.at[zo], line_in.at[zo], line_send.at[0], line_recv.at[0], {"seq": me + 2}
-        )
-
-    def skew_copy(zo):
-        return remote(
-            skew_out.at[zo], pair_in.at[zo], skew_send.at[0], pair_recv.at[0],
-            {"seq": partner + 2},
-        )
-
-    def gather(zo, device, out):
-        chosen = owned(device)
-        for yo in (0, 1):
-            for h in (0, 1):
-                out[zo, yo, h] = select(kv, (2 * zo + yo, h), chosen)
-
-    def pass_cache(zo):
-        @pl.when((zo == z) | takes_kv)
-        def _():
-            gather(zo, partner, pair_out)
-            pair_copy(zo).start()
-
-        @pl.when(hosts)
-        def _():
-            gather(zo, me + 2, line_out)
-            line_copy(zo).start()
-            gather(zo, partner + 2, skew_out)
-            skew_copy(zo).start()
-
     pairs = jnp.where(hosts, 2, 1)
 
     def phase(d, carry):
@@ -421,6 +463,10 @@
         def _():
             pass_cache(z - d + 1)
 
+        @pl.when(hosts & (d > 2) & (z - d + 1 >= 1))
+        def _():
+            lift_cache(z - d + 1)
+
         @pl.when(hosts & (d == jnp.minimum(2, z)))
         def _():
             settle(kv.at[2 * top :], lend_recv)
@@ -429,17 +475,17 @@
         def side(j, carry):
             @pl.when((z - d >= 0) & takes_kv)
             def _():
-                @pl.when(d > 1)
-                def _():
-                    take(d, j)
-
                 origin = 2 * (z - d) + jnp.where(j == 0, y, 1 - y)
-
-                def one(i, carry):
-                    attend(2 * i, origin, None)
-                    return carry
-
-                lax.fori_loop(0, pairs, one, 0)
+                for h, work in enumerate((weigh, mix)):
+                    pl.when(d > 1)(functools.partial(take, origin, h))
+
+                    def one(i, carry):
+                        work(i, origin)
+                        return carry
+
+                    lax.fori_loop(0, pairs, one, 0)
+                    if h == 0:
+                        pl.when((d == z) & (j == 1))(invert)
 
             return carry
 
@@ -447,6 +493,19 @@
         return carry
 
     lax.fori_loop(1, nz, phase, 0)
+
+    pl.when(z == 0)(invert)
+
+    @pl.when(frees)
+    def _():
+        settle(kv.at[: 2 * top - 2], z_send)
+        pl.semaphore_signal(turn, inc=1, device_id={"tp": sib}, device_id_type=MESH)
+
+    @pl.when(defers)
+    def _():
+        pl.semaphore_wait(turn, 1)
+        for h in (0, 1):
+            z_copy(1 - y, h).start()
 
     def rows_of(r):
         return pl.ds(pl.multiple_of(r * ROWS, ROWS), ROWS)
@@ -464,10 +523,11 @@
 
     def finish(s, r, out, lead):
         for hh in range(group):
-            out[(*lead, slice(None), slice(hh * HD, (hh + 1) * HD))] = (
-                acc[hh, s, rows_of(r), :]
-                / jnp.sum(den[hh, s, rows_of(r), :], axis=-1, keepdims=True)
-            ).astype(jnp.bfloat16)
+            for i in range(HD // LANES):
+                cols = slice(i * LANES, (i + 1) * LANES)
+                out[(*lead, slice(None), slice(hh * HD + i * LANES, hh * HD + (i + 1) * LANES))] = (
+                    acc[hh, s, rows_of(r), cols] * den[hh, s, rows_of(r), :]
+                ).astype(jnp.bfloat16)
 
     def away(r, carry):
         finish(1 - y, r, att_out, (r,))
@@ -484,9 +544,20 @@
             lent_copy(yq, r, y).start()
         return carry
 
+    def both_slabs(r, carry):
+        give(r, carry)
+        return away(r, carry)
+
+    @pl.when(hosts)
+    def _():
+        lax.fori_loop(0, chunks, both_slabs, 0)
+
+    @pl.when(jnp.logical_not(lends | hosts))
+    def _():
+        lax.fori_loop(0, chunks, away, 0)
+
     @pl.when(jnp.logical_not(lends))
     def _():
-        lax.fori_loop(0, chunks, away, 0)
         lax.fori_loop(0, chunks, home, 0)
 
     def rs_copy(kind, r, src, dst, recv, to):
@@ -505,8 +576,8 @@
         return jnp.dot(rows, wbuf[f, g], preferred_element_type=jnp.float32)
 
     def part(f, r):
-        pair = pl.ds(2 * r, 2)
-        rows = [att[g, pair].reshape(2 * ROWS, group_cols) for g in (0, 1)]
+        some = pl.ds(merge * r, merge)
+        rows = [att[g, some].reshape(LANES, group_cols) for g in (0, 1)]
         return product(rows[0], f, 0) + product(rows[1], f, 1)
 
     settle(wbuf, w_sem)
@@ -517,10 +588,6 @@
     def _():
         for i, f in enumerate(sent):
             early[i] = product(att[y].reshape(shard, group_cols), f, y)
-
-    @pl.when(hosts)
-    def _():
-        lax.fori_loop(0, chunks, give, 0)
 
     def send_sib(r):
         pl.when(jnp.logical_not(lends))(att_copy(r, 1 - y).wait_recv)
@@ -529,8 +596,7 @@
         def _():
             both_heads = att.at[:, r]
             pltpu.make_async_copy(both_heads, both_heads, att_recv.at[r]).wait()
-            for i, f in enumerate(sent):
-                early[i, rows_of(r), :] = product(att[y, r], f, y)
+            early[0, rows_of(r), :] = product(att[y, r], diagonal, y)
 
         to_sib[r] = (early[0, rows_of(r), :] + product(att[1 - y, r], diagonal, 1 - y)).astype(
             jnp.bfloat16
@@ -538,6 +604,10 @@
         sib_copy(r).start()
 
     def send_x(r):
+        @pl.when(lends)
+        def _():
+            early[1, rows_of(r), :] = product(att[y, r], across, y)
+
         mine = early[1, rows_of(r), :] + product(att[1 - y, r], across, 1 - y)
         sib_copy(r).wait_recv()
         to_x[r] = (mine + from_sib[r].astype(jnp.float32)).astype(jnp.bfloat16)
@@ -549,23 +619,24 @@
         return carry
 
     def third(r, carry):
-        pair = pl.ds(2 * r, 2)
-        to_sib2[pair] = part(sib, r).astype(jnp.bfloat16).reshape(2, ROWS, width)
-        for i in (0, 1):
-            sib2_copy(2 * r + i).start()
+        some = pl.ds(merge * r, merge)
+        to_sib2[some] = part(sib, r).astype(jnp.bfloat16).reshape(merge, ROWS, width)
+        for i in range(merge):
+            sib2_copy(merge * r + i).start()
         return carry
 
     def fourth(r, carry):
-        rows = pl.ds(pl.multiple_of(2 * r * ROWS, 2 * ROWS), 2 * ROWS)
+        rows = pl.ds(pl.multiple_of(r * LANES, LANES), LANES)
         total[rows, :] = part(t, r)
         return carry
 
     lax.fori_loop(0, chunks + 1, both, 0)
 
     pass_cache(0)
+    pl.when(hosts)(functools.partial(lift_cache, 0))
 
     for step in (third, fourth):
-        lax.fori_loop(0, chunks // 2, step, 0)
+        lax.fori_loop(0, chunks // merge, step, 0)
 
     mine_blocks = owned(me)
     local_row = lax.broadcasted_iota(jnp.int32, mine_blocks.shape, 0)
@@ -673,7 +744,7 @@
     settle(qpart, yq_send)
     for slab in range(nz):
 
-        @pl.when((z == slab) & sends_kv)
+        @pl.when((z == slab) & sends_kv & jnp.logical_not(frees))
         def _():
             settle(kv.at[: 2 * slab + 2], z_send)
 
@@ -751,6 +822,7 @@
             pltpu.VMEM((4, 2, group_cols, width), jnp.bfloat16),
             pltpu.VMEM((group_cols // HD, 4, shard, HD), jnp.float32),
             pltpu.VMEM((group_cols // HD, 4, shard, LANES), jnp.float32),
+            pltpu.VMEM((2, group_cols // HD, 2 * shard, HD), jnp.bfloat16),
             pltpu.VMEM((2, chunks, ROWS, group_cols), jnp.bfloat16),
             pltpu.VMEM((chunks, ROWS, group_cols), jnp.bfloat16),
             pltpu.VMEM((2, chunks, ROWS, group_cols), jnp.bfloat16),
@@ -785,6 +857,7 @@
             one,
             one,
             one,
+            pltpu.SemaphoreType.REGULAR,
         ],
         compiler_params=pltpu.CompilerParams(
             collective_id=0, has_side_effects=True, vmem_limit_bytes=62 * 1024 * 1024

time: 54.3 us -> 50.9 us (0.937)
  Pallas kernels: 52.8 us -> 49.4 us
    pallas_call x1, Pallas kernels: 51.7 us -> 48.3 us  [fused(): pl.pallas_call(functools.partial(layer_kernel, n), out_shape=(pltpu.VMEM(...]
where the time goes in v3:
time: 50.9 us; the launch traced here: 50.7 us
  Pallas kernels  49.4 us (97%)
  between operations  1.29 us (3%)
    pallas_call x1, Pallas kernels, fused(): pl.pallas_call(functools.partial(layer_kernel, n), out_shape=(pltpu.VMEM(...  48.3 us
    pallas_call x1, Pallas kernels, fused(): pl.pallas_call(put_out, out_shape=tuple((jax.ShapeDtypeStruct(a.shape, a....  1.15 us

profile of v3, /device:TPU:25, one launch (start us, length us, event | category | flops | bytes accessed | tf_op | source)
XLA Modules:
  0.0 50.7 jit_solution(7001037434651774212)
XLA Ops:
  1.3 48.3 %shard_map.103 = (bf16[256,896]{1,0:T(8,128)(2,1)S(1)}, bf16[512,512]{1,0:T(8,128)(2,1)S(1)}, bf16[512,512]{1,0:T(8,128)(2,1)S(1)}) custom-call(bf16[256,1024]{1,0:T(8,128)(2,1)} %bitcast.7, bf16[256,512]{1,0:T(8,128)(2,1)} %bitcast.9, bf16[256,512]{1,0:T(8,128)(2,1)} %bitcast.10, bf16[256,896]{1,0:T(8,128)(2,1)} %bitcast.8, f32[896]{0:T(1024)} %scale_hbm.1, ...), custom_call_target="tpu_custom_call" | custom-call | tf_op jit(solution)/shard_map/pallas_call | solution.py:802
  49.6 1.1 %shard_map.104 = (bf16[256,896]{1,0:T(8,128)(2,1)}, bf16[512,512]{1,0:T(8,128)(2,1)}, bf16[512,512]{1,0:T(8,128)(2,1)}) custom-call(bf16[256,896]{1,0:T(8,128)(2,1)S(1)} %get-tuple-element.9.refs_0_, bf16[512,512]{1,0:T(8,128)(2,1)S(1)} %get-tuple-element.10.refs_1_, bf16[512,512]{1,0:T(8,128)(2,1)S(1)} %get-tuple-element.11.refs_2_), custom_call_target="tpu_custom_call" | custom-call | tf_op jit(solution)/shard_map/pallas_call | solution.py:870

commit v4 on v3

--- a/solution.py
+++ b/solution.py
@@ -155,7 +155,7 @@
     to_sib, to_x, to_sib2, from_sib, from_x, from_sib2, early, total, folds, sq_out, sq_in,
     in_sem, w_sem, y_send, yq_send, y_recv, z_send, z_recv, lend_recv, q_send, q_recv, lent_send,
     down_send, down_recv, pair_send, pair_recv, line_send, line_recv, skew_send, att_send, att_recv,
-    rs_send, rs_recv, sib2_recv, sq_send, sq_recv, turn,
+    rs_send, rs_recv, sib2_recv, sq_send, sq_recv, turn, lower, upper,
 ):
     nz = n // 2
     top = nz - 1
@@ -202,10 +202,12 @@
     barrier = pltpu.get_barrier_semaphore()
     for peer in (sib, across, diagonal):
         pl.semaphore_signal(barrier, inc=1, device_id={"tp": peer}, device_id_type=MESH)
-    for hop in range(1, n):
-        pl.semaphore_signal(
-            barrier, inc=1, device_id={"seq": lax.rem(me + hop, n)}, device_id_type=MESH
-        )
+    pl.semaphore_signal(barrier, inc=1, device_id={"seq": partner}, device_id_type=MESH)
+    for there, peer in ((z < top, me + 2), (z > 0, me - 2)):
+
+        @pl.when(there)
+        def _():
+            pl.semaphore_signal(barrier, inc=1, device_id={"seq": peer}, device_id_type=MESH)
 
     def clear(s, carry):
         acc[s] = jnp.zeros(acc.shape[1:], jnp.float32)
@@ -213,7 +215,7 @@
         return carry
 
     lax.fori_loop(0, acc.shape[0], clear, 0)
-    pl.semaphore_wait(barrier, n + 2)
+    pl.semaphore_wait(barrier, 4 + jnp.where(z < top, 1, 0) + jnp.where(z > 0, 1, 0))
 
     def remote(src, dst, send, recv, to):
         return pltpu.make_async_remote_copy(
@@ -286,6 +288,18 @@
     for load in loads[7:]:
         load.start()
 
+    @pl.when(z > 0)
+    def _():
+        pl.semaphore_wait(lower, 1)
+
+    @pl.when(z < top)
+    def _():
+        pl.semaphore_signal(lower, inc=1, device_id={"seq": me + 2}, device_id_type=MESH)
+
+    @pl.when(lends)
+    def _():
+        pl.semaphore_signal(upper, inc=1, device_id={"seq": me - 2}, device_id_type=MESH)
+
     def owned(device):
         block = own_ref[0, 0] * 0
         for b in range(n):
@@ -362,7 +376,10 @@
         pl.when(lends)(lend_kv(partner, h).start)
     lax.fori_loop(0, 2 * z, post, 0)
 
-    pl.when(hosts)(functools.partial(lift_cache, z))
+    @pl.when(hosts)
+    def _():
+        pl.semaphore_wait(upper, 1)
+        lift_cache(z)
 
     def take(origin, h):
         z_copy(origin, h).wait_recv()
@@ -456,57 +473,6 @@
 
         lax.fori_loop(0, 2, one, 0)
 
-    pairs = jnp.where(hosts, 2, 1)
-
-    def phase(d, carry):
-        @pl.when(z - d + 1 >= 1)
-        def _():
-            pass_cache(z - d + 1)
-
-        @pl.when(hosts & (d > 2) & (z - d + 1 >= 1))
-        def _():
-            lift_cache(z - d + 1)
-
-        @pl.when(hosts & (d == jnp.minimum(2, z)))
-        def _():
-            settle(kv.at[2 * top :], lend_recv)
-            own_slab(2, top)
-
-        def side(j, carry):
-            @pl.when((z - d >= 0) & takes_kv)
-            def _():
-                origin = 2 * (z - d) + jnp.where(j == 0, y, 1 - y)
-                for h, work in enumerate((weigh, mix)):
-                    pl.when(d > 1)(functools.partial(take, origin, h))
-
-                    def one(i, carry):
-                        work(i, origin)
-                        return carry
-
-                    lax.fori_loop(0, pairs, one, 0)
-                    if h == 0:
-                        pl.when((d == z) & (j == 1))(invert)
-
-            return carry
-
-        lax.fori_loop(0, 2, side, 0)
-        return carry
-
-    lax.fori_loop(1, nz, phase, 0)
-
-    pl.when(z == 0)(invert)
-
-    @pl.when(frees)
-    def _():
-        settle(kv.at[: 2 * top - 2], z_send)
-        pl.semaphore_signal(turn, inc=1, device_id={"tp": sib}, device_id_type=MESH)
-
-    @pl.when(defers)
-    def _():
-        pl.semaphore_wait(turn, 1)
-        for h in (0, 1):
-            z_copy(1 - y, h).start()
-
     def rows_of(r):
         return pl.ds(pl.multiple_of(r * ROWS, ROWS), ROWS)
 
@@ -529,35 +495,82 @@
                     acc[hh, s, rows_of(r), cols] * den[hh, s, rows_of(r), :]
                 ).astype(jnp.bfloat16)
 
-    def away(r, carry):
-        finish(1 - y, r, att_out, (r,))
-        att_copy(r, y).start()
-        return carry
-
-    def home(r, carry):
-        finish(y, r, att, (y, r))
-        return carry
-
     def give(r, carry):
         for yq in (1 - y, y):
             finish(2 + yq, r, lent_out, (yq, r))
             lent_copy(yq, r, y).start()
         return carry
 
-    def both_slabs(r, carry):
-        give(r, carry)
-        return away(r, carry)
-
-    @pl.when(hosts)
-    def _():
-        lax.fori_loop(0, chunks, both_slabs, 0)
-
-    @pl.when(jnp.logical_not(lends | hosts))
+    pairs = jnp.where(hosts, 2, 1)
+
+    def phase(d, carry):
+        @pl.when(z - d + 1 >= 1)
+        def _():
+            pass_cache(z - d + 1)
+
+        @pl.when(hosts & (d > 2) & (z - d + 1 >= 1))
+        def _():
+            lift_cache(z - d + 1)
+
+        @pl.when(hosts & (d == jnp.minimum(2, z)))
+        def _():
+            settle(kv.at[2 * top :], lend_recv)
+            own_slab(2, top)
+
+        def side(j, carry):
+            @pl.when((z - d >= 0) & takes_kv)
+            def _():
+                origin = 2 * (z - d) + jnp.where(j == 0, y, 1 - y)
+                for h, work in enumerate((weigh, mix)):
+                    pl.when(d > 1)(functools.partial(take, origin, h))
+
+                    def one(i, carry):
+                        which = pairs - 1 - i
+                        work(which, origin)
+                        if h == 1:
+
+                            @pl.when((which == 1) & (d == z) & (j == 1))
+                            def _():
+                                lax.fori_loop(0, chunks, give, 0)
+
+                        return carry
+
+                    lax.fori_loop(0, pairs, one, 0)
+                    if h == 0:
+                        pl.when((d == z) & (j == 1))(invert)
+
+            return carry
+
+        lax.fori_loop(0, 2, side, 0)
+        return carry
+
+    lax.fori_loop(1, nz, phase, 0)
+
+    pl.when(z == 0)(invert)
+
+    @pl.when(frees)
+    def _():
+        settle(kv.at[: 2 * top - 2], z_send)
+        pl.semaphore_signal(turn, inc=1, device_id={"tp": sib}, device_id_type=MESH)
+
+    @pl.when(defers)
+    def _():
+        pl.semaphore_wait(turn, 1)
+        for h in (0, 1):
+            z_copy(1 - y, h).start()
+
+    def away(r, carry):
+        finish(1 - y, r, att_out, (r,))
+        att_copy(r, y).start()
+        return carry
+
+    def home(r, carry):
+        finish(y, r, att, (y, r))
+        return carry
+
+    @pl.when(jnp.logical_not(lends))
     def _():
         lax.fori_loop(0, chunks, away, 0)
-
-    @pl.when(jnp.logical_not(lends))
-    def _():
         lax.fori_loop(0, chunks, home, 0)
 
     def rs_copy(kind, r, src, dst, recv, to):
@@ -858,6 +871,8 @@
             one,
             one,
             pltpu.SemaphoreType.REGULAR,
+            pltpu.SemaphoreType.REGULAR,
+            pltpu.SemaphoreType.REGULAR,
         ],
         compiler_params=pltpu.CompilerParams(
             collective_id=0, has_side_effects=True, vmem_limit_bytes=62 * 1024 * 1024

time: 50.9 us -> 49.8 us (0.978)
  Pallas kernels: 49.4 us -> 48.3 us
    pallas_call x1, Pallas kernels: 48.3 us -> 47.2 us  [fused(): pl.pallas_call(functools.partial(layer_kernel, n), out_shape=(pltpu.VMEM(...]
where the time goes in v4:
time: 49.8 us; the launch traced here: 49.6 us
  Pallas kernels  48.3 us (97%)
  between operations  1.29 us (3%)
    pallas_call x1, Pallas kernels, fused(): pl.pallas_call(functools.partial(layer_kernel, n), out_shape=(pltpu.VMEM(...  47.2 us
    pallas_call x1, Pallas kernels, fused(): pl.pallas_call(put_out, out_shape=tuple((jax.ShapeDtypeStruct(a.shape, a....  1.15 us

profile of v4, /device:TPU:25, one launch (start us, length us, event | category | flops | bytes accessed | tf_op | source)
XLA Modules:
  0.0 49.6 jit_solution(16110921482232109651)
XLA Ops:
  1.3 47.2 %shard_map.103 = (bf16[256,896]{1,0:T(8,128)(2,1)S(1)}, bf16[512,512]{1,0:T(8,128)(2,1)S(1)}, bf16[512,512]{1,0:T(8,128)(2,1)S(1)}) custom-call(bf16[256,1024]{1,0:T(8,128)(2,1)} %bitcast.7, bf16[256,512]{1,0:T(8,128)(2,1)} %bitcast.9, bf16[256,512]{1,0:T(8,128)(2,1)} %bitcast.10, bf16[256,896]{1,0:T(8,128)(2,1)} %bitcast.8, f32[896]{0:T(1024)} %scale_hbm.1, ...), custom_call_target="tpu_custom_call" | custom-call | tf_op jit(solution)/shard_map/pallas_call | solution.py:815
  48.5 1.1 %shard_map.104 = (bf16[256,896]{1,0:T(8,128)(2,1)}, bf16[512,512]{1,0:T(8,128)(2,1)}, bf16[512,512]{1,0:T(8,128)(2,1)}) custom-call(bf16[256,896]{1,0:T(8,128)(2,1)S(1)} %get-tuple-element.9.refs_0_, bf16[512,512]{1,0:T(8,128)(2,1)S(1)} %get-tuple-element.10.refs_1_, bf16[512,512]{1,0:T(8,128)(2,1)S(1)} %get-tuple-element.11.refs_2_), custom_call_target="tpu_custom_call" | custom-call | tf_op jit(solution)/shard_map/pallas_call | solution.py:885

commit v5 on v4

--- a/solution.py
+++ b/solution.py
@@ -14,6 +14,7 @@
 LOG2E = 1.4426950408889634
 ROWS = 32
 LANES = 128
+PIECES = 4
 
 
 soft_cap = 50.0
@@ -790,13 +791,15 @@
 
 def put_out(*refs):
     count = (len(refs) - 1) // 2
-    copies = [
-        pltpu.make_async_copy(refs[i], refs[count + i], refs[-1].at[i]) for i in range(count)
-    ]
-    for copy in copies:
-        copy.start()
-    for copy in copies:
-        copy.wait()
+    sems = refs[-1]
+    for i in range(count):
+        src, dst = refs[i], refs[count + i]
+        step = src.shape[0] // PIECES
+        for k in range(PIECES):
+            rows = pl.ds(k * step, step)
+            pltpu.make_async_copy(src.at[rows], dst.at[rows], sems.at[i]).start()
+    for i in range(count):
+        pltpu.make_async_copy(refs[i], refs[count + i], sems.at[i]).wait()
 
 
 def fused(n, queries, key_rows, value_rows, residual, out_weight, post_scale, lengths, owners):

time: 49.8 us -> 49.8 us (level)
  no operation moved by 1% of the time
where the time goes in v5:
time: 49.8 us; the launch traced here: 49.6 us
  Pallas kernels  48.3 us (97%)
  between operations  1.29 us (3%)
    pallas_call x1, Pallas kernels, fused(): pl.pallas_call(functools.partial(layer_kernel, n), out_shape=(pltpu.VMEM(...  47.2 us
    pallas_call x1, Pallas kernels, fused(): pl.pallas_call(put_out, out_shape=tuple((jax.ShapeDtypeStruct(a.shape, a....  1.13 us

profile of v5, /device:TPU:25, one launch (start us, length us, event | category | flops | bytes accessed | tf_op | source)
XLA Modules:
  0.0 49.6 jit_solution(354932078893581017)
XLA Ops:
  1.3 47.2 %shard_map.103 = (bf16[256,896]{1,0:T(8,128)(2,1)S(1)}, bf16[512,512]{1,0:T(8,128)(2,1)S(1)}, bf16[512,512]{1,0:T(8,128)(2,1)S(1)}) custom-call(bf16[256,1024]{1,0:T(8,128)(2,1)} %bitcast.7, bf16[256,512]{1,0:T(8,128)(2,1)} %bitcast.9, bf16[256,512]{1,0:T(8,128)(2,1)} %bitcast.10, bf16[256,896]{1,0:T(8,128)(2,1)} %bitcast.8, f32[896]{0:T(1024)} %scale_hbm.1, ...), custom_call_target="tpu_custom_call" | custom-call | tf_op jit(solution)/shard_map/pallas_call | solution.py:818
  48.5 1.1 %shard_map.104 = (bf16[256,896]{1,0:T(8,128)(2,1)}, bf16[512,512]{1,0:T(8,128)(2,1)}, bf16[512,512]{1,0:T(8,128)(2,1)}) custom-call(bf16[256,896]{1,0:T(8,128)(2,1)S(1)} %get-tuple-element.9.refs_0_, bf16[512,512]{1,0:T(8,128)(2,1)S(1)} %get-tuple-element.10.refs_1_, bf16[512,512]{1,0:T(8,128)(2,1)S(1)} %get-tuple-element.11.refs_2_), custom_call_target="tpu_custom_call" | custom-call | tf_op jit(solution)/shard_map/pallas_call | solution.py:888
